TPU v7x, 256 devices: a whole 4x4x8 slice. The times are simulated.
256 devices in a mesh: row: 8 (over z_lo, x), col: 32 (over y, z_hi, core).
Axes of the slice: x: 4, y: 4, z: 8 (z_hi: 4, z_lo: 2; z = z_hi * 2 + z_lo), core: 2. Of those that a mesh axis runs over, the one named last changes fastest.
Arguments:
- matrix: bfloat16 [4096, 131072], P('row', 'col'), may hold values from -0.09375 to 0.09375
- measured: float32 [256, 4096], P(None, 'row'), may hold values from -160 to 160
- support: int32 [4, 2048], replicated, may hold values from 0 to 131071, as said below
Outputs:
- estimate: float32 [256, 131072], P('row', 'col')
- row_norms: float32 [131072], P('col')
- residual_energy: float32 [4], replicated
Inputs may be any that keep to these rules, and one draw needn't show every extreme that they name: Each row of support lists 2048 distinct signal-row indices in increasing order; in every row, each aligned block of 4096 indices (the signal rows of one index of col) holds at most 128 of them, and some block exactly 128.
All inputs are finite; a program needn't handle non-finite values.
Results may differ from a plain program's by a relative error of at most 0.015.
Values may be sent and summed in bfloat16 or wider, within the bound.
A program may use at most 64 MiB of HBM per device.

v0:
```python
import jax
import jax.numpy as jnp
from jax import lax
from jax.sharding import Mesh
from jax.sharding import PartitionSpec as P

KMAX = 128
COL = ("col_0", "col_1", "col_2")


STEP_SIZE = 0.25


def split_up(shard, dim, length):
    before, after = (shard.shape[:dim], shard.shape[dim + 1 :])
    return jnp.moveaxis(shard.reshape(*before, length, -1, *after), dim, 0)


def sent_and_summed(shard, axis, dim):
    tiles = split_up(shard, dim, lax.axis_size(axis))
    arrived = lax.all_to_all(tiles, axis, split_axis=0, concat_axis=0, tiled=True)
    return arrived.astype(jnp.float32).sum(axis=0)


def in_order(tiles, dim):
    tiles = jnp.moveaxis(tiles, 0, dim)
    lengths = tiles.shape
    return tiles.reshape(*lengths[:dim], lengths[dim] * lengths[dim + 1], *lengths[dim + 2 :])


def sent_to_all(shard, axis):
    copies = jnp.broadcast_to(shard, (lax.axis_size(axis), *shard.shape))
    return lax.all_to_all(copies, axis, split_axis=0, concat_axis=0, tiled=True)


def collect(shard, axis, dim):
    return in_order(sent_to_all(shard, axis), dim)


def sum_by_axis(shard, axes, dim):
    far, near = axes
    own = sent_and_summed(split_up(shard, dim, lax.axis_size(far)), near, dim + 1)
    return jnp.sum(
        lax.all_to_all(own.astype(jnp.bfloat16), far, 0, 0, tiled=True).astype(jnp.float32), axis=0
    )


def rows_for(lines, length):
    spare = -len(lines) % length
    return jnp.pad(lines, [(0, spare)] + [(0, 0)] * (lines.ndim - 1))


def gather_axes(shard, axes, dim):
    far, near = axes
    tiles = sent_to_all(sent_to_all(shard, far), near)
    return in_order(tiles.swapaxes(0, 1).reshape(-1, *shard.shape), dim)


def total_of(shard, axes):
    lines = shard.reshape(-1, shard.shape[-1])
    own = sum_by_axis(rows_for(lines, lax.axis_size(axes[0]) * lax.axis_size(axes[1])), axes, 0)
    whole = gather_axes(own.astype(jnp.bfloat16), axes, 0)
    return whole[: len(lines)].reshape(shard.shape).astype(jnp.float32)


def over_copies(shard, axis):
    everything = sent_to_all(shard, axis)
    return jnp.sum(everything, axis=0)


def together(arrays, axis):
    vector, at, done = (jnp.concatenate([a.reshape(-1) for a in arrays]), 0, [])
    so_far = over_copies(vector, axis)
    for a in arrays:
        done.append(so_far[at : at + a.size].reshape(a.shape))
        at += a.size
    return tuple(done)


def local_support(support_row, start_col, block_width):
    below_count = jnp.sum((support_row < start_col).astype(jnp.int32))
    inside = jnp.sum(
        ((support_row >= start_col) & (support_row < start_col + block_width)).astype(jnp.int32)
    )
    padded = jnp.concatenate([support_row, jnp.full((KMAX,), start_col + block_width, jnp.int32)])
    window = lax.dynamic_slice_in_dim(padded, below_count, KMAX) - start_col
    occupied = jnp.arange(KMAX) < inside
    take_index = jnp.where(occupied, window, 0)
    drop_index = jnp.where(occupied, window, block_width)
    return (take_index, drop_index, occupied)


def dense_step(current, residual_half, matrix, drop_index):
    gradient = sent_and_summed(
        jnp.dot(residual_half, matrix, preferred_element_type=jnp.float32).astype(jnp.bfloat16),
        "row",
        0,
    )
    stepped = current + STEP_SIZE * gradient
    keep_mask = jnp.zeros((current.shape[1],), jnp.float32).at[drop_index].set(1.0, mode="drop")
    return (stepped, stepped * keep_mask[None, :])


def kept_step(current, residual_half, matrix, take_index, drop_index, occupied):
    kept_matrix = jnp.where(
        occupied[None, :], jnp.take(matrix, take_index, axis=1), jnp.zeros((), jnp.bfloat16)
    )
    kept_slope = sent_and_summed(
        jnp.dot(residual_half, kept_matrix, preferred_element_type=jnp.float32).astype(
            jnp.bfloat16
        ),
        "row",
        0,
    )
    updated = jnp.take(current, take_index, axis=1) + STEP_SIZE * kept_slope
    return jnp.zeros_like(current).at[:, drop_index].set(updated, mode="drop")


def local(matrix, measured, support):
    signals = measured.shape[0]
    rows_mine = signals // lax.axis_size("row")
    columns = matrix.shape[1]
    offset = lax.axis_index(COL) * columns
    iterations = support.shape[0]
    total_count = signals * measured.shape[1] * lax.axis_size("row")
    current = jnp.zeros((rows_mine, columns), jnp.float32)
    stepped = current
    residual_terms = []
    for iteration in range(iterations):
        if iteration == 0:
            residual = measured
        else:
            current_half = current.astype(jnp.bfloat16)
            take_before, drop_before, occupied_before = local_support(
                support[iteration - 1], offset, columns
            )
            kept_matrix = jnp.where(
                occupied_before[None, :],
                jnp.take(matrix, take_before, axis=1),
                jnp.zeros((), jnp.bfloat16),
            )
            kept_current = jnp.take(current_half, take_before, axis=1)
            partial_image = lax.dot_general(
                collect(kept_current, "row", 0),
                kept_matrix,
                (((1,), (1,)), ((), ())),
                preferred_element_type=jnp.float32,
            )
            predicted = total_of(partial_image.astype(jnp.bfloat16), (("col_0", "col_1"), "col_2"))
            residual = measured - predicted
        local_energy = jnp.sum(residual * residual)
        residual_terms.append(local_energy)
        residual_half = residual.astype(jnp.bfloat16)
        take_index, drop_index, occupied = local_support(support[iteration], offset, columns)
        final_pass = iteration == iterations - 1
        if final_pass:
            stepped, current = dense_step(current, residual_half, matrix, drop_index)
        else:
            current = kept_step(current, residual_half, matrix, take_index, drop_index, occupied)
    row_local = jnp.sum(stepped * stepped, axis=0)
    column_energy, residual_sums = together((row_local, jnp.stack(residual_terms)), "row")
    return (current, jnp.sqrt(column_energy), residual_sums / total_count)


def solution(mesh):
    torus = Mesh(
        mesh.devices.reshape(mesh.shape["row"], 4, 4, 2), ("row", "col_0", "col_1", "col_2")
    )
    placed = (P("row", COL), P(None, "row"), P())
    return jax.shard_map(
        local, mesh=torus, in_specs=placed, out_specs=(P("row", COL), P(COL), P()), check_vma=False
    )
```

profile of v0, /device:TPU:32, one launch (start us, length us, event | category | flops | bytes accessed | tf_op | source)
XLA Modules:
  0.0 269.6 jit_solution(17653099352199669644)
XLA Ops:
  5.6 6.5 %copy.92 = bf16[512,4096]{0,1:T(8,128)(2,1)} copy(bf16[512,4096]{1,0:T(8,128)(2,1)} %param.9) | data formatting | bytes 8388608 | tf_op args[0]
  12.2 3.6 %gather_fusion.1 = bf16[128,512]{1,0:T(8,128)(2,1)S(1)} fusion(bf16[512,4096]{0,1:T(8,128)(2,1)} %copy.92, s32[1024]{0:T(1024)S(1)} %pad_clamp_fusion.2), kind=kCustom, calls=%fused_computation.1.clone | custom fusion | bytes 262656 | tf_op jit(solution)/shard_map/jit(_take)/gather | solution.py:106
  16.8 5.8 %all-to-all-start = ((bf16[8,32,128]{2,1,0:T(8,128)(2,1)}), bf16[8,32,128]{2,1,0:T(8,128)(2,1)S(1)}, u32[]{:S(2)}, u32[]{:S(2)}) async-start(bf16[8,32,128]{2,1,0:T(8,128)(2,1)} %bitcast.6), calls=%async_computation | async-start | bytes 131072 | tf_op jit(solution)/shard_map/all_to_all | solution.py:21
  32.3 8.8 %all_to_all.101 = bf16[8,32,128]{2,1,0:T(8,128)(2,1)S(1)} all-to-all(bf16[8,32,128]{2,1,0:T(8,128)(2,1)S(1)} %broadcast_in_dim.144), channel_id=1, replica_groups=mesh['row'=8,'col_0'=4,'col_1'=4,'col_2'=2] {'row'}, dimensions={0} | all-to-all | bytes 131072 | tf_op jit(solution)/shard_map/all_to_all | solution.py:33
  41.4 3.9 %all_to_all.102 = bf16[2,16,8,512]{3,2,1,0:T(8,128)(2,1)S(1)} all-to-all(bf16[2,16,8,512]{3,2,1,0:T(8,128)(2,1)S(1)} %bitcast.98), channel_id=1, replica_groups=mesh['row'=8,'col_0'=4,'col_1'=4,'col_2'=2] {'col_2'}, dimensions={0} | all-to-all | bytes 524288 | tf_op jit(solution)/shard_map/all_to_all | solution.py:21
  46.1 10.3 %all-to-all-start.3 = ((bf16[16,8,512]{2,1,0:T(8,128)(2,1)}), bf16[16,8,512]{2,1,0:T(8,128)(2,1)S(1)}, u32[]{:S(2)}, u32[]{:S(2)}) async-start(bf16[16,8,512]{2,1,0:T(8,128)(2,1)} %reduce_sum.265), calls=%async_computation.3 | async-start | bytes 262144 | tf_op jit(solution)/shard_map/all_to_all | solution.py:44
  59.1 8.5 %all-to-all-done.3 = bf16[16,8,512]{2,1,0:T(8,128)(2,1)S(1)} async-done(((bf16[16,8,512]{2,1,0:T(8,128)(2,1)}), bf16[16,8,512]{2,1,0:T(8,128)(2,1)S(1)}, u32[]{:S(2)}, u32[]{:S(2)}) %all-to-all-start.3) | async-done | bytes 131104 | tf_op jit(solution)/shard_map/all_to_all | solution.py:44
  68.3 3.5 %all-to-all-start.4 = ((bf16[16,8,512]{2,1,0:T(8,128)(2,1)}), bf16[16,8,512]{2,1,0:T(8,128)(2,1)S(1)}, u32[]{:S(2)}, u32[]{:S(2)}) async-start(bf16[16,8,512]{2,1,0:T(8,128)(2,1)} %broadcast_in_dim.145), calls=%async_computation.4 | async-start | bytes 262144 | tf_op jit(solution)/shard_map/all_to_all | solution.py:33
  72.5 3.6 %gather_fusion.4 = bf16[128,512]{1,0:T(8,128)(2,1)S(1)} fusion(bf16[512,4096]{0,1:T(8,128)(2,1)} %copy.92, s32[1024]{0:T(1024)S(1)} %pad_clamp_fusion.1), kind=kCustom, calls=%fused_computation.5.clone | custom fusion | bytes 262656 | tf_op jit(solution)/shard_map/jit(_take)/gather | solution.py:106
  76.8 5.6 %all-to-all-done.4 = bf16[16,8,512]{2,1,0:T(8,128)(2,1)S(1)} async-done(((bf16[16,8,512]{2,1,0:T(8,128)(2,1)}), bf16[16,8,512]{2,1,0:T(8,128)(2,1)S(1)}, u32[]{:S(2)}, u32[]{:S(2)}) %all-to-all-start.4) | async-done | bytes 131104 | tf_op jit(solution)/shard_map/all_to_all | solution.py:33
  82.5 3.9 %all_to_all.103 = bf16[2,16,8,512]{3,2,1,0:T(8,128)(2,1)S(1)} all-to-all(bf16[2,16,8,512]{3,2,1,0:T(8,128)(2,1)S(1)} %broadcast_in_dim.146), channel_id=1, replica_groups=mesh['row'=8,'col_0'=4,'col_1'=4,'col_2'=2] {'col_2'}, dimensions={0} | all-to-all | bytes 524288 | tf_op jit(solution)/shard_map/all_to_all | solution.py:33
  87.5 4.4 %all-to-all-start.6 = ((bf16[8,32,128]{2,1,0:T(8,128)(2,1)}), bf16[8,32,128]{2,1,0:T(8,128)(2,1)S(1)}, u32[]{:S(2)}, u32[]{:S(2)}) async-start(bf16[8,32,128]{2,1,0:T(8,128)(2,1)} %bitcast.16), calls=%async_computation.6 | async-start | bytes 131072 | tf_op jit(solution)/shard_map/all_to_all | solution.py:21
  93.3 3.6 %all-to-all-done.6 = bf16[8,32,128]{2,1,0:T(8,128)(2,1)S(1)} async-done(((bf16[8,32,128]{2,1,0:T(8,128)(2,1)}), bf16[8,32,128]{2,1,0:T(8,128)(2,1)S(1)}, u32[]{:S(2)}, u32[]{:S(2)}) %all-to-all-start.6) | async-done | bytes 65568 | tf_op jit(solution)/shard_map/all_to_all | solution.py:21
  101.7 8.7 %all_to_all.104 = bf16[8,32,128]{2,1,0:T(8,128)(2,1)S(1)} all-to-all(bf16[8,32,128]{2,1,0:T(8,128)(2,1)S(1)} %broadcast_in_dim.148), channel_id=1, replica_groups=mesh['row'=8,'col_0'=4,'col_1'=4,'col_2'=2] {'row'}, dimensions={0} | all-to-all | bytes 131072 | tf_op jit(solution)/shard_map/all_to_all | solution.py:33
  110.8 3.9 %all_to_all.105 = bf16[2,16,8,512]{3,2,1,0:T(8,128)(2,1)S(1)} all-to-all(bf16[2,16,8,512]{3,2,1,0:T(8,128)(2,1)S(1)} %bitcast.99), channel_id=1, replica_groups=mesh['row'=8,'col_0'=4,'col_1'=4,'col_2'=2] {'col_2'}, dimensions={0} | all-to-all | bytes 524288 | tf_op jit(solution)/shard_map/all_to_all | solution.py:21
  115.5 3.9 %all-to-all-start.9 = ((bf16[16,8,512]{2,1,0:T(8,128)(2,1)}), bf16[16,8,512]{2,1,0:T(8,128)(2,1)S(1)}, u32[]{:S(2)}, u32[]{:S(2)}) async-start(bf16[16,8,512]{2,1,0:T(8,128)(2,1)} %reduce_sum.268), calls=%async_computation.9 | async-start | bytes 262144 | tf_op jit(solution)/shard_map/all_to_all | solution.py:44
  121.0 9.5 %all-to-all-done.9 = bf16[16,8,512]{2,1,0:T(8,128)(2,1)S(1)} async-done(((bf16[16,8,512]{2,1,0:T(8,128)(2,1)}), bf16[16,8,512]{2,1,0:T(8,128)(2,1)S(1)}, u32[]{:S(2)}, u32[]{:S(2)}) %all-to-all-start.9) | async-done | bytes 131104 | tf_op jit(solution)/shard_map/all_to_all | solution.py:44
  131.3 3.5 %all-to-all-start.10 = ((bf16[16,8,512]{2,1,0:T(8,128)(2,1)}), bf16[16,8,512]{2,1,0:T(8,128)(2,1)S(1)}, u32[]{:S(2)}, u32[]{:S(2)}) async-start(bf16[16,8,512]{2,1,0:T(8,128)(2,1)} %broadcast_in_dim.149), calls=%async_computation.10 | async-start | bytes 262144 | tf_op jit(solution)/shard_map/all_to_all | solution.py:33
  135.6 3.6 %gather_fusion.7 = bf16[128,512]{1,0:T(8,128)(2,1)S(1)} fusion(bf16[512,4096]{0,1:T(8,128)(2,1)} %copy.92, s32[1024]{0:T(1024)S(1)} %pad_clamp_fusion), kind=kCustom, calls=%fused_computation.6.clone | custom fusion | bytes 262656 | tf_op jit(solution)/shard_map/jit(_take)/gather | solution.py:106
  139.9 5.5 %all-to-all-done.10 = bf16[16,8,512]{2,1,0:T(8,128)(2,1)S(1)} async-done(((bf16[16,8,512]{2,1,0:T(8,128)(2,1)}), bf16[16,8,512]{2,1,0:T(8,128)(2,1)S(1)}, u32[]{:S(2)}, u32[]{:S(2)}) %all-to-all-start.10) | async-done | bytes 131104 | tf_op jit(solution)/shard_map/all_to_all | solution.py:33
  145.4 3.9 %all_to_all.106 = bf16[2,16,8,512]{3,2,1,0:T(8,128)(2,1)S(1)} all-to-all(bf16[2,16,8,512]{3,2,1,0:T(8,128)(2,1)S(1)} %broadcast_in_dim.150), channel_id=1, replica_groups=mesh['row'=8,'col_0'=4,'col_1'=4,'col_2'=2] {'col_2'}, dimensions={0} | all-to-all | bytes 524288 | tf_op jit(solution)/shard_map/all_to_all | solution.py:33
  151.3 4.4 %all-to-all-start.12 = ((bf16[8,32,128]{2,1,0:T(8,128)(2,1)}), bf16[8,32,128]{2,1,0:T(8,128)(2,1)S(1)}, u32[]{:S(2)}, u32[]{:S(2)}) async-start(bf16[8,32,128]{2,1,0:T(8,128)(2,1)} %bitcast.26), calls=%async_computation.12 | async-start | bytes 131072 | tf_op jit(solution)/shard_map/all_to_all | solution.py:21
  157.1 3.6 %all-to-all-done.12 = bf16[8,32,128]{2,1,0:T(8,128)(2,1)S(1)} async-done(((bf16[8,32,128]{2,1,0:T(8,128)(2,1)}), bf16[8,32,128]{2,1,0:T(8,128)(2,1)S(1)}, u32[]{:S(2)}, u32[]{:S(2)}) %all-to-all-start.12) | async-done | bytes 65568 | tf_op jit(solution)/shard_map/all_to_all | solution.py:21
  165.5 8.7 %all_to_all.107 = bf16[8,32,128]{2,1,0:T(8,128)(2,1)S(1)} all-to-all(bf16[8,32,128]{2,1,0:T(8,128)(2,1)S(1)} %broadcast_in_dim.152), channel_id=1, replica_groups=mesh['row'=8,'col_0'=4,'col_1'=4,'col_2'=2] {'row'}, dimensions={0} | all-to-all | bytes 131072 | tf_op jit(solution)/shard_map/all_to_all | solution.py:33
  174.6 3.9 %all_to_all.108 = bf16[2,16,8,512]{3,2,1,0:T(8,128)(2,1)S(1)} all-to-all(bf16[2,16,8,512]{3,2,1,0:T(8,128)(2,1)S(1)} %bitcast.100), channel_id=1, replica_groups=mesh['row'=8,'col_0'=4,'col_1'=4,'col_2'=2] {'col_2'}, dimensions={0} | all-to-all | bytes 524288 | tf_op jit(solution)/shard_map/all_to_all | solution.py:21
  178.6 15.0 %all_to_all.109 = bf16[16,8,512]{2,1,0:T(8,128)(2,1)S(1)} all-to-all(bf16[16,8,512]{2,1,0:T(8,128)(2,1)S(1)} %reduce_sum.271), channel_id=1, replica_groups=mesh['row'=8,'col_0'=4,'col_1'=4,'col_2'=2] {'col_0','col_1'}, dimensions={0} | all-to-all | bytes 262144 | tf_op jit(solution)/shard_map/all_to_all | solution.py:44
  193.6 13.4 %all_to_all.110 = bf16[16,8,512]{2,1,0:T(8,128)(2,1)S(1)} all-to-all(bf16[16,8,512]{2,1,0:T(8,128)(2,1)S(1)} %broadcast_in_dim.153), channel_id=1, replica_groups=mesh['row'=8,'col_0'=4,'col_1'=4,'col_2'=2] {'col_0','col_1'}, dimensions={0} | all-to-all | bytes 262144 | tf_op jit(solution)/shard_map/all_to_all | solution.py:33
  207.1 3.9 %all_to_all.111 = bf16[2,16,8,512]{3,2,1,0:T(8,128)(2,1)S(1)} all-to-all(bf16[2,16,8,512]{3,2,1,0:T(8,128)(2,1)S(1)} %broadcast_in_dim.154), channel_id=1, replica_groups=mesh['row'=8,'col_0'=4,'col_1'=4,'col_2'=2] {'col_2'}, dimensions={0} | all-to-all | bytes 524288 | tf_op jit(solution)/shard_map/all_to_all | solution.py:33
  212.0 4.7 %convolution_convert_fusion = bf16[256,4096]{1,0:T(8,128)(2,1)} fusion(bf16[512,4096]{1,0:T(8,128)(2,1)} %param.9, bf16[256,512]{1,0:T(8,128)(2,1)S(1)} %bitcast_subtract_fusion), kind=kOutput, calls=%fused_computation.13 | convolution fusion | flops 1074790400 | bytes 6553600 | tf_op jit(solution)/shard_map/dot_general | solution.py:95
  216.7 5.4 %all-to-all-start.18 = ((bf16[8,32,4096]{2,1,0:T(8,128)(2,1)}), bf16[8,32,4096]{2,1,0:T(8,128)(2,1)}, u32[]{:S(2)}, u32[]{:S(2)}) async-start(bf16[8,32,4096]{2,1,0:T(8,128)(2,1)} %bitcast.94), calls=%async_computation.18 | async-start | bytes 4194304 | tf_op jit(solution)/shard_map/all_to_all | solution.py:21
  227.9 20.5 %all-to-all-done.18 = bf16[8,32,4096]{2,1,0:T(8,128)(2,1)} async-done(((bf16[8,32,4096]{2,1,0:T(8,128)(2,1)}), bf16[8,32,4096]{2,1,0:T(8,128)(2,1)}, u32[]{:S(2)}, u32[]{:S(2)}) %all-to-all-start.18) | async-done | bytes 2097184 | tf_op jit(solution)/shard_map/all_to_all | solution.py:21
  259.0 4.2 %all-to-all-start.19 = ((f32[8,1,4100]{2,1,0:T(1,128)}), f32[8,1,4100]{2,1,0:T(1,128)S(1)}, u32[]{:S(2)}, u32[]{:S(2)}) async-start(f32[8,1,4100]{2,1,0:T(1,128)} %broadcast_in_dim.158), calls=%async_computation.19 | async-start | bytes 270336 | tf_op jit(solution)/shard_map/all_to_all | solution.py:33
  (98 shorter events, 58.4 us)
Async XLA Ops:
  5.6 10.1 %copy-start = (f32[256,512]{1,0:T(8,128)S(1)}, f32[256,512]{1,0:T(8,128)}, u32[]{:S(2)}) copy-start(f32[256,512]{1,0:T(8,128)} %param.10) | copy-start | bytes 1572868
  16.8 10.7 %all-to-all-start = ((bf16[8,32,128]{2,1,0:T(8,128)(2,1)}), bf16[8,32,128]{2,1,0:T(8,128)(2,1)S(1)}, u32[]{:S(2)}, u32[]{:S(2)}) async-start(bf16[8,32,128]{2,1,0:T(8,128)(2,1)} %bitcast.6), calls=%async_computation | async-start | bytes 131072 | tf_op jit(solution)/shard_map/all_to_all | solution.py:21
  46.1 21.5 %all-to-all-start.3 = ((bf16[16,8,512]{2,1,0:T(8,128)(2,1)}), bf16[16,8,512]{2,1,0:T(8,128)(2,1)S(1)}, u32[]{:S(2)}, u32[]{:S(2)}) async-start(bf16[16,8,512]{2,1,0:T(8,128)(2,1)} %reduce_sum.265), calls=%async_computation.3 | async-start | bytes 262144 | tf_op jit(solution)/shard_map/all_to_all | solution.py:44
  68.3 14.2 %all-to-all-start.4 = ((bf16[16,8,512]{2,1,0:T(8,128)(2,1)}), bf16[16,8,512]{2,1,0:T(8,128)(2,1)S(1)}, u32[]{:S(2)}, u32[]{:S(2)}) async-start(bf16[16,8,512]{2,1,0:T(8,128)(2,1)} %broadcast_in_dim.145), calls=%async_computation.4 | async-start | bytes 262144 | tf_op jit(solution)/shard_map/all_to_all | solution.py:33
  87.5 9.4 %all-to-all-start.6 = ((bf16[8,32,128]{2,1,0:T(8,128)(2,1)}), bf16[8,32,128]{2,1,0:T(8,128)(2,1)S(1)}, u32[]{:S(2)}, u32[]{:S(2)}) async-start(bf16[8,32,128]{2,1,0:T(8,128)(2,1)} %bitcast.16), calls=%async_computation.6 | async-start | bytes 131072 | tf_op jit(solution)/shard_map/all_to_all | solution.py:21
  115.5 15.1 %all-to-all-start.9 = ((bf16[16,8,512]{2,1,0:T(8,128)(2,1)}), bf16[16,8,512]{2,1,0:T(8,128)(2,1)S(1)}, u32[]{:S(2)}, u32[]{:S(2)}) async-start(bf16[16,8,512]{2,1,0:T(8,128)(2,1)} %reduce_sum.268), calls=%async_computation.9 | async-start | bytes 262144 | tf_op jit(solution)/shard_map/all_to_all | solution.py:44
  131.3 14.2 %all-to-all-start.10 = ((bf16[16,8,512]{2,1,0:T(8,128)(2,1)}), bf16[16,8,512]{2,1,0:T(8,128)(2,1)S(1)}, u32[]{:S(2)}, u32[]{:S(2)}) async-start(bf16[16,8,512]{2,1,0:T(8,128)(2,1)} %broadcast_in_dim.149), calls=%async_computation.10 | async-start | bytes 262144 | tf_op jit(solution)/shard_map/all_to_all | solution.py:33
  149.4 0.8 copy-start.1
  151.3 9.4 %all-to-all-start.12 = ((bf16[8,32,128]{2,1,0:T(8,128)(2,1)}), bf16[8,32,128]{2,1,0:T(8,128)(2,1)S(1)}, u32[]{:S(2)}, u32[]{:S(2)}) async-start(bf16[8,32,128]{2,1,0:T(8,128)(2,1)} %bitcast.26), calls=%async_computation.12 | async-start | bytes 131072 | tf_op jit(solution)/shard_map/all_to_all | solution.py:21
  211.1 0.8 copy-start.2
  216.7 31.6 %all-to-all-start.18 = ((bf16[8,32,4096]{2,1,0:T(8,128)(2,1)}), bf16[8,32,4096]{2,1,0:T(8,128)(2,1)}, u32[]{:S(2)}, u32[]{:S(2)}) async-start(bf16[8,32,4096]{2,1,0:T(8,128)(2,1)} %bitcast.94), calls=%async_computation.18 | async-start | bytes 4194304 | tf_op jit(solution)/shard_map/all_to_all | solution.py:21
  259.0 9.4 %all-to-all-start.19 = ((f32[8,1,4100]{2,1,0:T(1,128)}), f32[8,1,4100]{2,1,0:T(1,128)S(1)}, u32[]{:S(2)}, u32[]{:S(2)}) async-start(f32[8,1,4100]{2,1,0:T(1,128)} %broadcast_in_dim.158), calls=%async_computation.19 | async-start | bytes 270336 | tf_op jit(solution)/shard_map/all_to_all | solution.py:33
where the time goes:
time: 273 us; the launch traced here: 270 us
  blocking collectives  78.3 us (29%)
  waiting for transfers between devices  62.6 us (23%)
  starting transfers between devices  45.4 us (17%)
  local copies, waits for them, and re-layouts  44.9 us (16%)
  other arithmetic  22.1 us (8%)
  between operations  8.53 us (3%)
  matrix products  7.74 us (3%)
    all_to_all x7, blocking collectives, sent_to_all(): return lax.all_to_all(copies, axis, split_axis=0, concat_axis=0, tiled=True)  51.5 us
    all_to_all x4, waiting for transfers between devices, sent_and_summed(): lax.all_to_all(tiles, axis, split_axis=0, concat_axis=0, tiled=True)  31.1 us
    all_to_all x4, starting transfers between devices, sent_and_summed(): lax.all_to_all(tiles, axis, split_axis=0, concat_axis=0, tiled=True)  20.1 us
    all_to_all x2, waiting for transfers between devices, sum_by_axis(): lax.all_to_all(own.astype(jnp.bfloat16), far, 0, 0, tiled=True)  18 us
    all_to_all x1, blocking collectives, sum_by_axis(): lax.all_to_all(own.astype(jnp.bfloat16), far, 0, 0, tiled=True)  15 us
    all_to_all x2, starting transfers between devices, sum_by_axis(): lax.all_to_all(own.astype(jnp.bfloat16), far, 0, 0, tiled=True)  14.2 us
    all_to_all x3, waiting for transfers between devices, sent_to_all(): return lax.all_to_all(copies, axis, split_axis=0, concat_axis=0, tiled=True)  13.5 us
    all_to_all x3, blocking collectives, sent_and_summed(): lax.all_to_all(tiles, axis, split_axis=0, concat_axis=0, tiled=True)  11.8 us
  transfers between devices with their start and end apart: 9, of which 9 were waited for; matrix products, arithmetic and copies ran while one was open for 8% of the time, Pallas kernels for 0%

commit v1 on v0

v1 whole, which is shorter than its diff:
```python
import functools

import jax
import jax.numpy as jnp
from jax import lax
from jax.experimental import pallas as pl
from jax.experimental.pallas import tpu as pltpu
from jax.sharding import PartitionSpec as P

KMAX = 128
STEP_SIZE = 0.25
CORES = 2
NEAR = (((1,), (1,)), ((), ()))
F32 = jnp.float32
BF16 = jnp.bfloat16


def iota(shape, dim):
    return lax.broadcasted_iota(jnp.int32, shape, dim)


def window(line, start, width):
    count = line.shape[1]
    below = jnp.sum(jnp.where(line < start, 1.0, 0.0), axis=1, keepdims=True)
    upto = jnp.sum(jnp.where(line < start + width, 1.0, 0.0), axis=1, keepdims=True)
    place = iota((KMAX, count), 1) - iota((KMAX, count), 0)
    local = (line - start).astype(F32)
    found = jnp.sum(
        jnp.where(place == below.astype(jnp.int32), local, 0.0), axis=1, keepdims=True
    )
    there = iota((KMAX, 1), 0).astype(F32) < upto - below
    return jnp.where(there, found, -1.0).astype(jnp.int32)


def one_hot(index, first, width):
    return jnp.where(iota((KMAX, width), 1) + first == index, 1.0, 0.0)


def split3(value):
    high = value.astype(BF16)
    rest = value - high.astype(F32)
    middle = rest.astype(BF16)
    low = (rest - middle.astype(F32)).astype(BF16)
    return jnp.concatenate([high, middle, low], axis=0)


def add3(value):
    third = value.shape[0] // 3
    return value[:third] + value[third : 2 * third] + value[2 * third :]


def kernel(
    shape,
    support,
    measured,
    matrix,
    estimate,
    norms,
    energies,
    a_block,
    index_own,
    index_held,
    image,
    kept,
    first_send,
    first_recv,
    slope_send,
    slope_recv,
    current_all,
    held,
    seen_all,
    moved_send,
    moved_recv,
    residual_all,
    grad_send,
    grad_recv,
    norm_all,
    load_sem,
    send_sem,
    recv_sem,
    grad_ssem,
    grad_rsem,
):
    rows, far, high, total_count = shape
    width = matrix.shape[1]
    depth = matrix.shape[0]
    group = measured.shape[0] // rows
    steps = support.shape[0]
    chunk = grad_send.shape[3]
    chunks = width // chunk
    i = lax.axis_index("row")
    col = lax.axis_index("col")
    core = lax.rem(col, CORES)
    h = lax.rem(col // CORES, high)
    y = col // (CORES * high)
    q = y * CORES + core

    def at(yy, hh, cc):
        return (yy * high + hh) * CORES + cc

    def member(k):
        return at(k // CORES, h, lax.rem(k, CORES))

    sems = iter(range(1000))
    pending = []

    def remote(src, dst, where, slot):
        return pltpu.make_async_remote_copy(
            src_ref=src,
            dst_ref=dst,
            send_sem=send_sem.at[slot],
            recv_sem=recv_sem.at[slot],
            device_id=where,
            device_id_type=pl.DeviceIdType.MESH,
        )

    row_peers = [(lax.rem(i + d, rows), col) for d in range(1, rows)]
    y_peers = [(i, at(lax.rem(y + d, far), h, core)) for d in range(1, far)]
    y_from = [lax.rem(y - d + far, far) for d in range(1, far)]
    h_peers = [(i, at(y, lax.rem(h + d, high), core)) for d in range(1, high)]
    h_from = [lax.rem(h - d + high, high) for d in range(1, high)]
    partner = (i, at(y, h, 1 - core))

    barrier = pltpu.get_barrier_semaphore()
    for peer in row_peers + y_peers + h_peers + [partner]:
        pl.semaphore_signal(
            barrier, inc=1, device_id=peer, device_id_type=pl.DeviceIdType.MESH
        )
    on_diagonal = i == q
    for k in range(rows):

        @pl.when(jnp.logical_not(jnp.logical_and(on_diagonal, i == k)))
        def _():
            pl.semaphore_signal(
                barrier,
                inc=1,
                device_id=(k, member(i)),
                device_id_type=pl.DeviceIdType.MESH,
            )

    loads = [
        pltpu.make_async_copy(
            matrix.at[:, pl.ds(c * chunk, chunk)],
            a_block.at[:, pl.ds(c * chunk, chunk)],
            load_sem.at[c],
        )
        for c in range(chunks)
    ]
    for load in loads:
        load.start()

    for t in range(steps):
        index_own[t] = window(support[t : t + 1, :], col * width, width)

    image[...] = jnp.zeros_like(image)
    for c in range(chunks):
        loads[c].wait()
        hot = jnp.concatenate(
            [one_hot(index_own[t], c * chunk, chunk).astype(BF16) for t in range(steps - 1)],
            axis=0,
        )
        image[...] += lax.dot_general(
            hot, a_block[:, c * chunk : (c + 1) * chunk], NEAR, preferred_element_type=F32
        )
    for t in range(steps - 1):
        kept[t, q] = image[t * KMAX : (t + 1) * KMAX, :].astype(BF16)

    first = lax.dot_general(
        measured[...].astype(BF16), kept[0, q], NEAR, preferred_element_type=F32
    ).astype(BF16)
    for k in range(rows):
        first_send[k] = first[k * group : (k + 1) * group, :]

    pl.semaphore_wait(barrier, len(row_peers + y_peers + h_peers) + 1 + rows - jnp.where(on_diagonal, 1, 0))

    base = [next(sems) for _ in range(rows)]
    first_copies = []
    for k in range(rows):
        copy = pltpu.make_async_remote_copy(
            src_ref=first_send.at[k],
            dst_ref=first_recv.at[i],
            send_sem=send_sem.at[base[k]],
            recv_sem=recv_sem.at[i],
            device_id=(q, member(k)),
            device_id_type=pl.DeviceIdType.MESH,
        )
        other = jnp.logical_not(jnp.logical_and(on_diagonal, q == k))
        pl.when(other)(copy.start)

        @pl.when(jnp.logical_not(other))
        def _():
            first_recv[i] = first_send[k]

        first_copies.append((other, copy))

    spread = []
    for t in range(steps - 1):
        to_y = [
            remote(kept.at[t, q], kept.at[t, q], peer, next(sems)) for peer in y_peers
        ]
        to_partner = remote(kept.at[t, q], kept.at[t, q], partner, next(sems))
        relay_slots = [next(sems) for _ in y_peers]
        for copy in to_y:
            copy.start()
        to_partner.start()
        pending += to_y + [to_partner]
        spread.append((to_y, to_partner, relay_slots))

    def gather(t, buffer, parts):
        to_y, to_partner, relay_slots = parts
        relays = []
        for n, copy in enumerate(to_y):
            copy.wait_recv()
            slot = y_from[n] * CORES + core
            relay = remote(buffer.at[slot], buffer.at[slot], partner, relay_slots[n])
            relay.start()
            relays.append(relay)
        to_partner.wait_recv()
        for relay in relays:
            relay.wait_recv()
        pending.extend(relays)

    for t in range(steps - 1):
        index_held[t] = window(support[t : t + 1, :], member(i) * width, width)

    def carried(t, value):
        diagonal = iota((KMAX, KMAX), 0) == iota((KMAX, KMAX), 1)
        after = jnp.sum(
            jnp.where(diagonal, index_held[t + 1].astype(F32), 0.0), axis=0, keepdims=True
        ).astype(jnp.int32)
        before = index_held[t]
        same = jnp.where(jnp.logical_and(before == after, before >= 0), 1.0, 0.0).astype(BF16)
        return add3(jnp.dot(split3(value), same, preferred_element_type=F32))

    for k in range(rows):
        self_here = jnp.logical_and(on_diagonal, i == k)
        arrived = pltpu.make_async_remote_copy(
            src_ref=first_send.at[k],
            dst_ref=first_recv.at[k],
            send_sem=send_sem.at[base[k]],
            recv_sem=recv_sem.at[k],
            device_id=(q, member(k)),
            device_id_type=pl.DeviceIdType.MESH,
        )
        pl.when(jnp.logical_not(self_here))(arrived.wait_recv)
    current = STEP_SIZE * jnp.sum(first_recv[...].astype(F32), axis=0)

    own_measured = measured[pl.ds(pl.multiple_of(q * group, group), group), :]
    energy = [jnp.sum(own_measured * own_measured)]
    for t in range(steps - 1):
        if t > 0:
            gather(t, kept.at[t], spread[t])
            slope = lax.dot_general(
                residual.astype(BF16),
                kept[t].reshape(rows * KMAX, depth),
                NEAR,
                preferred_element_type=F32,
            ).astype(BF16)
            for k in range(rows):
                slope_send[t - 1, k] = slope[:, k * KMAX : (k + 1) * KMAX]
            copies = []
            for d, peer in enumerate(row_peers):
                copies.append(
                    remote(
                        slope_send.at[t - 1, peer[0]], slope_recv.at[t - 1, d], peer, next(sems)
                    )
                )
                copies[-1].start()
            carry = carried(t - 1, held[...])
            for copy in copies:
                copy.wait_recv()
            pending += copies
            gathered = slope_send[t - 1, i].astype(F32) + jnp.sum(
                slope_recv[t - 1].astype(F32), axis=0
            )
            current = carry + STEP_SIZE * gathered
        held[...] = current
        current_all[t, i] = current.astype(BF16)
        copies = [
            remote(current_all.at[t, i], current_all.at[t, i], peer, next(sems))
            for peer in row_peers
        ]
        for copy in copies:
            copy.start()
        pending += copies
        if t == steps - 2:
            moved_send[...] = current
            move = remote(moved_send, moved_recv, (q, member(i)), next(sems))
            pl.when(jnp.logical_not(on_diagonal))(move.start)

            @pl.when(on_diagonal)
            def _():
                moved_recv[...] = moved_send[...]

        if t == 0:
            gather(t, kept.at[t], spread[t])
        for copy in copies:
            copy.wait_recv()
        signals = jnp.concatenate([current_all[t, k] for k in range(rows)], axis=1)
        seen_all[t, h] = jnp.dot(
            signals, kept[t].reshape(rows * KMAX, depth), preferred_element_type=F32
        ).astype(BF16)
        copies = [
            remote(seen_all.at[t, h], seen_all.at[t, h], peer, next(sems)) for peer in h_peers
        ]
        for copy in copies:
            copy.start()
        for copy in copies:
            copy.wait_recv()
        pending += copies
        residual = own_measured - jnp.sum(seen_all[t].astype(F32), axis=0)
        energy.append(jnp.sum(residual * residual))

    lanes = iota((16, depth), 1)
    values = jnp.zeros((16, depth), F32)
    for t in range(steps):
        values = jnp.where(lanes == t, energy[t], values)
    top = values.astype(BF16).astype(F32)
    mid = (values - top).astype(BF16).astype(F32)
    low = values - top - mid
    line = iota((16, depth), 0)
    values = jnp.where(line == 0, top, jnp.where(line == 1, mid, jnp.where(line == 2, low, 0.0)))
    residual_all[q] = jnp.concatenate([residual.astype(BF16), values.astype(BF16)], axis=0)
    to_y = [remote(residual_all.at[q], residual_all.at[q], peer, next(sems)) for peer in y_peers]
    to_partner = remote(residual_all.at[q], residual_all.at[q], partner, next(sems))
    for copy in to_y:
        copy.start()
    to_partner.start()
    pending += to_y + [to_partner]
    gather(0, residual_all, (to_y, to_partner, [next(sems) for _ in y_peers]))

    energy_rows = jnp.sum(
        jnp.sum(residual_all[:, group:, :KMAX].astype(F32), axis=0), axis=0, keepdims=True
    )
    norm_all[i, :, width:] = energy_rows

    all_signals = jnp.concatenate([residual_all[k, :group, :] for k in range(rows)], axis=0)

    def grad_copy(c, d):
        peer = row_peers[d]
        return pltpu.make_async_remote_copy(
            src_ref=grad_send.at[c, peer[0]],
            dst_ref=grad_recv.at[c, d],
            send_sem=grad_ssem.at[c, d],
            recv_sem=grad_rsem.at[c, d],
            device_id=peer,
            device_id_type=pl.DeviceIdType.MESH,
        )

    for c in range(chunks):
        part = jnp.dot(
            all_signals, a_block[:, c * chunk : (c + 1) * chunk], preferred_element_type=F32
        ).astype(BF16)
        for k in range(rows):
            grad_send[c, k] = part[k * group : (k + 1) * group, :]
        for d in range(rows - 1):
            grad_copy(c, d).start()

    pl.when(jnp.logical_not(on_diagonal))(move.wait_recv)
    moved = split3(moved_recv[...])
    for c in range(chunks):
        span = slice(c * chunk, (c + 1) * chunk)
        before = add3(
            jnp.dot(
                moved,
                one_hot(index_own[steps - 2], c * chunk, chunk).astype(BF16),
                preferred_element_type=F32,
            )
        )
        mask = jnp.sum(one_hot(index_own[steps - 1], c * chunk, chunk), axis=0, keepdims=True)
        gradient = grad_send[c, i].astype(F32)
        for d in range(rows - 1):
            grad_copy(c, d).wait_recv()
            gradient += grad_recv[c, d].astype(F32)
        stepped = before + STEP_SIZE * gradient
        estimate[:, span] = stepped * mask
        norm_all[i, :, span] = jnp.sum(stepped * stepped, axis=0, keepdims=True)

    copies = [remote(norm_all.at[i], norm_all.at[i], peer, next(sems)) for peer in row_peers]
    for copy in copies:
        copy.start()
    for copy in copies:
        copy.wait_recv()
    pending += copies
    summed = jnp.sum(norm_all[...], axis=0)
    norms[...] = jnp.sqrt(summed[:, :width])
    energies[...] = summed[:, width:] / total_count

    for other, copy in first_copies:
        pl.when(other)(copy.wait_send)
    pl.when(jnp.logical_not(on_diagonal))(move.wait_send)
    for copy in pending:
        copy.wait_send()
    for c in range(chunks):
        for d in range(rows - 1):
            grad_copy(c, d).wait_send()


def solution(mesh, far=4, high=4, chunk=512):
    rows = mesh.shape["row"]

    def local(matrix, measured, support):
        depth, width = matrix.shape
        signals = measured.shape[0]
        group = signals // rows
        steps = support.shape[0]
        turns = steps - 1
        span = min(chunk, width)
        chunks = width // span
        estimate, norms, energies = pl.pallas_call(
            functools.partial(
                kernel, (rows, far, high, float(signals * depth * rows))
            ),
            out_shape=(
                jax.ShapeDtypeStruct((group, width), F32),
                jax.ShapeDtypeStruct((1, width), F32),
                jax.ShapeDtypeStruct((1, KMAX), F32),
            ),
            in_specs=[
                pl.BlockSpec(memory_space=pltpu.VMEM),
                pl.BlockSpec(memory_space=pltpu.VMEM),
                pl.BlockSpec(memory_space=pl.ANY),
            ],
            out_specs=(pl.BlockSpec(memory_space=pltpu.VMEM),) * 3,
            scratch_shapes=[
                pltpu.VMEM((depth, width), BF16),
                pltpu.VMEM((steps, KMAX, 1), jnp.int32),
                pltpu.VMEM((turns, KMAX, 1), jnp.int32),
                pltpu.VMEM((turns * KMAX, depth), F32),
                pltpu.VMEM((turns, rows, KMAX, depth), BF16),
                pltpu.VMEM((rows, group, KMAX), BF16),
                pltpu.VMEM((rows, group, KMAX), BF16),
                pltpu.VMEM((turns, rows, group, KMAX), BF16),
                pltpu.VMEM((turns, rows - 1, group, KMAX), BF16),
                pltpu.VMEM((turns, rows, group, KMAX), BF16),
                pltpu.VMEM((group, KMAX), F32),
                pltpu.VMEM((turns, high, group, depth), BF16),
                pltpu.VMEM((group, KMAX), F32),
                pltpu.VMEM((group, KMAX), F32),
                pltpu.VMEM((rows, group + 16, depth), BF16),
                pltpu.VMEM((chunks, rows, group, span), BF16),
                pltpu.VMEM((chunks, rows - 1, group, span), BF16),
                pltpu.VMEM((rows, 1, width + KMAX), F32),
                pltpu.SemaphoreType.DMA((chunks,)),
                pltpu.SemaphoreType.DMA((120,)),
                pltpu.SemaphoreType.DMA((120,)),
                pltpu.SemaphoreType.DMA((chunks, rows - 1)),
                pltpu.SemaphoreType.DMA((chunks, rows - 1)),
            ],
            compiler_params=pltpu.CompilerParams(
                collective_id=0, has_side_effects=True, vmem_limit_bytes=56 * 2**20
            ),
        )(support, measured, matrix)
        return estimate, norms.reshape(width), energies[0, :steps]

    return jax.shard_map(
        local,
        mesh=mesh,
        in_specs=(P("row", "col"), P(None, "row"), P()),
        out_specs=(P("row", "col"), P("col"), P()),
        check_vma=False,
    )
```

time: 273 us -> 105 us (0.38)
  Pallas kernels: 0 us -> 98.4 us
  blocking collectives: 78.3 us -> 0 us
  waiting for transfers between devices: 62.6 us -> 0 us
  starting transfers between devices: 45.4 us -> 0 us
  local copies, waits for them, and re-layouts: 44.9 us -> 4.37 us
  other arithmetic: 22.1 us -> 0 us
  between operations: 8.53 us -> 0.64 us
  matrix products: 7.74 us -> 0 us
    pallas_call x0 -> x1, Pallas kernels: none -> 98.4 us  [local(): pl.pallas_call(functools.partial(kernel, (rows, far, high, float(signals...]
    all_to_all x11 -> x0, blocking collectives: 78.3 us -> none  [the longest x7 51.5 us: sent_to_all(): return lax.all_to_all(copies, axis, split_axis=0, concat_axis=0, tiled=True)]
    all_to_all x9 -> x0, waiting for transfers between devices: 62.6 us -> none  [the longest x4 31.1 us: sent_and_summed(): lax.all_to_all(tiles, axis, split_axis=0, concat_axis=0, tiled=True)]
    all_to_all x9 -> x0, starting transfers between devices: 45.4 us -> none  [the longest x4 20.1 us: sent_and_summed(): lax.all_to_all(tiles, axis, split_axis=0, concat_axis=0, tiled=True)]
    gather x12 -> x0, local copies, waits for them, and re-layouts: 18.9 us -> none  [the longest x3 10.8 us: kept_step(): jnp.take(matrix, take_index, axis=1)]
    reduce_sum x15 -> x0, other arithmetic: 10.6 us -> none  [the longest x1 3.43 us: local(): row_local = jnp.sum(stepped * stepped, axis=0)]
    unnamed x8 -> x2, local copies, waits for them, and re-layouts: 11.1 us -> 3.19 us
    dot_general x7 -> x0, matrix products: 7.74 us -> none  [the longest x1 4.74 us: dense_step(): jnp.dot(residual_half, matrix, preferred_element_type=jnp.float32)]
  transfers between devices with their start and end apart: 9 -> 0, of which waited for: 9 -> 0; matrix products, arithmetic and copies ran while one was open for 8% -> 0% of each run, Pallas kernels for 0% -> 0%
where the time goes in v1:
time: 105 us; the launch traced here: 103 us
  Pallas kernels  98.4 us (94%)
  local copies, waits for them, and re-layouts  4.37 us (4%)
    pallas_call x1, Pallas kernels, local(): pl.pallas_call(functools.partial(kernel, (rows, far, high, float(signals...  98.4 us
    unnamed x2, local copies, waits for them, and re-layouts  3.19 us

profile of v1, /device:TPU:32, one launch (start us, length us, event | category | flops | bytes accessed | tf_op | source)
XLA Modules:
  0.0 103.5 jit_solution(12540144924612134876)
XLA Ops:
  0.6 98.4 %shard_map.58 = (f32[32,4096]{1,0:T(8,128)}, f32[1,4096]{1,0:T(1,128)}, f32[1,128]{1,0:T(1,128)}) custom-call(s32[4,2048]{1,0:T(4,128)} %support.1, f32[256,512]{1,0:T(8,128)} %measured.1, bf16[512,4096]{1,0:T(8,128)(2,1)} %matrix.1), custom_call_target="tpu_custom_call" | custom-call | tf_op jit(solution)/shard_map/pallas_call | solution.py:410
  99.1 1.2 %slice_bitcast_fusion = f32[4]{0:T(128)} fusion(f32[1,128]{1,0:T(1,128)} %get-tuple-element.8), kind=kLoop, calls=%fused_computation | loop fusion | bytes 32 | tf_op jit(solution)/shard_map/squeeze | solution.py:454
  100.3 1.9 %copy.8 = f32[32,4096]{1,0:T(8,128)} copy(f32[32,4096]{1,0:T(8,128)} %get-tuple-element.12) | data formatting | bytes 1048576
  102.1 1.3 %copy.9 = f32[4096]{0:T(1024)} copy(f32[4096]{0:T(1024)} %bitcast.3) | data formatting | bytes 32768

commit v2 on v1

v2 whole, which is shorter than its diff:
```python
import functools

import jax
import jax.numpy as jnp
from jax import lax
from jax.experimental import pallas as pl
from jax.experimental.pallas import tpu as pltpu
from jax.sharding import PartitionSpec as P

KMAX = 128
STEP_SIZE = 0.25
CORES = 2
NEAR = (((1,), (1,)), ((), ()))
F32 = jnp.float32
BF16 = jnp.bfloat16


def iota(shape, dim):
    return lax.broadcasted_iota(jnp.int32, shape, dim)


def window(line, start, width):
    count = line.shape[1]
    below = jnp.sum(jnp.where(line < start, 1.0, 0.0), axis=1, keepdims=True)
    upto = jnp.sum(jnp.where(line < start + width, 1.0, 0.0), axis=1, keepdims=True)
    place = iota((KMAX, count), 1) - iota((KMAX, count), 0)
    local = (line - start).astype(F32)
    found = jnp.sum(
        jnp.where(place == below.astype(jnp.int32), local, 0.0), axis=1, keepdims=True
    )
    there = iota((KMAX, 1), 0).astype(F32) < upto - below
    return jnp.where(there, found, -1.0).astype(jnp.int32)


def one_hot(index, first, width):
    return jnp.where(iota((KMAX, width), 1) + first == index, 1.0, 0.0)


def split3(value):
    high = value.astype(BF16)
    rest = value - high.astype(F32)
    middle = rest.astype(BF16)
    low = (rest - middle.astype(F32)).astype(BF16)
    return jnp.concatenate([high, middle, low], axis=0)


def add3(value):
    third = value.shape[0] // 3
    return value[:third] + value[third : 2 * third] + value[2 * third :]


def kernel(
    shape,
    support_in,
    measured_in,
    matrix,
    kept_out,
    sums_out,
    support,
    measured,
    a_block,
    index_own,
    index_held,
    image,
    kept,
    first_send,
    first_recv,
    slope_send,
    slope_recv,
    current_all,
    held,
    seen_all,
    moved_send,
    moved_recv,
    residual_all,
    grad_send,
    by_x,
    by_z,
    pair_send,
    pair_recv,
    line_send,
    line_recv,
    norm_all,
    load_sem,
    send_sem,
    recv_sem,
):
    rows, far, high, along_x = shape
    pairs = rows // 2
    depth, width = matrix.shape
    group = measured.shape[0] // rows
    steps = support.shape[0]
    chunk = grad_send.shape[3]
    chunks = width // chunk
    i = lax.axis_index("row")
    col = lax.axis_index("col")
    x = lax.rem(i, pairs)
    z = i // pairs
    core = lax.rem(col, CORES)
    h = lax.rem(col // CORES, high)
    y = col // (CORES * high)
    q = y * CORES + core
    sending = iter(range(send_sem.shape[0]))
    landing = iter(range(recv_sem.shape[0]))
    sent = []

    def at(yy, hh, cc):
        return (yy * high + hh) * CORES + cc

    def member(k):
        return at(k // CORES, h, lax.rem(k, CORES))

    def far_first(count):
        return sorted(range(1, count), key=lambda d: -min(d, count - d))

    def remote(src, dst, where, out, back):
        return pltpu.make_async_remote_copy(
            src_ref=src,
            dst_ref=dst,
            send_sem=send_sem.at[out],
            recv_sem=recv_sem.at[back],
            device_id=where,
            device_id_type=pl.DeviceIdType.MESH,
        )

    def await_all(sems, slot, ref):
        pltpu.make_async_copy(ref, ref, sems.at[slot]).wait()

    x_shift = far_first(pairs)
    offsets = [(1, d) for d in x_shift] + [(0, d) for d in x_shift] + [(1, 0)]
    row_peers = [
        (lax.rem(z + dz, 2) * pairs + lax.rem(x + dx, pairs), col) for dz, dx in offsets
    ]
    x_peers = [(z * pairs + lax.rem(x + d, pairs), col) for d in x_shift]
    across = ((1 - z) * pairs + x, col)
    y_shift = far_first(far)
    y_peers = [(i, at(lax.rem(y + d, far), h, core)) for d in y_shift]
    y_from = [lax.rem(y - d + far, far) for d in y_shift]
    h_peers = [(i, at(y, lax.rem(h + d, high), core)) for d in far_first(high)]
    partner = (i, at(y, h, 1 - core))

    barrier = pltpu.get_barrier_semaphore()
    for peer in row_peers + y_peers + h_peers + [partner]:
        pl.semaphore_signal(
            barrier, inc=1, device_id=peer, device_id_type=pl.DeviceIdType.MESH
        )
    on_diagonal = i == q
    off_diagonal = jnp.logical_not(on_diagonal)
    for k in range(rows):

        @pl.when(jnp.logical_or(off_diagonal, i != k))
        def _():
            pl.semaphore_signal(
                barrier,
                inc=1,
                device_id=(k, member(i)),
                device_id_type=pl.DeviceIdType.MESH,
            )

    support_load = pltpu.make_async_copy(support_in, support, load_sem.at[chunks])
    support_load.start()
    loads = [
        pltpu.make_async_copy(
            matrix.at[:, pl.ds(c * chunk, chunk)],
            a_block.at[:, pl.ds(c * chunk, chunk)],
            load_sem.at[c],
        )
        for c in range(chunks)
    ]
    for load in loads:
        load.start()
    measured_load = pltpu.make_async_copy(measured_in, measured, load_sem.at[chunks + 1])
    measured_load.start()
    support_load.wait()

    def find_own(t):
        index_own[t] = window(support[t : t + 1, :], col * width, width)

    def pick(first, last, loaded):
        total = jnp.zeros(((last - first) * KMAX, depth), F32)
        for c in range(chunks):
            if not loaded:
                loads[c].wait()
            hot = jnp.concatenate(
                [one_hot(index_own[t], c * chunk, chunk).astype(BF16) for t in range(first, last)],
                axis=0,
            )
            total += lax.dot_general(
                hot, a_block[:, c * chunk : (c + 1) * chunk], NEAR, preferred_element_type=F32
            )
        for t in range(first, last):
            kept[t, q] = total[(t - first) * KMAX : (t - first + 1) * KMAX, :].astype(BF16)

    find_own(0)
    pick(0, 1, False)
    measured_load.wait()

    first = lax.dot_general(
        measured[...].astype(BF16), kept[0, q], NEAR, preferred_element_type=F32
    ).astype(BF16)
    for k in range(rows):
        first_send[k] = first[k * group : (k + 1) * group, :]

    pl.semaphore_wait(
        barrier,
        len(row_peers + y_peers + h_peers) + 1 + rows - jnp.where(on_diagonal, 1, 0),
    )

    first_out, first_back = next(sending), next(landing)
    for k in range(rows):
        copy = remote(
            first_send.at[k], first_recv.at[i], (q, member(k)), first_out, first_back
        )
        other = jnp.logical_or(off_diagonal, q != k)
        pl.when(other)(copy.start)

        @pl.when(jnp.logical_not(other))
        def _():
            first_recv[i] = first_send[k]

    def spread(buffer):
        own = buffer.at[q]
        out, back = next(sending), next(landing)
        to_y = [remote(own, own, peer, out, next(landing)) for peer in y_peers]
        for copy in to_y:
            copy.start()
        remote(own, own, partner, out, back).start()
        sent.append((out, buffer.at[pl.ds(0, rows - 1)]))
        return to_y, out, back

    def relay(buffer, parts):
        to_y, out, back = parts
        for n, copy in enumerate(to_y):
            copy.wait_recv()
            slot = buffer.at[y_from[n] * CORES + core]
            remote(slot, slot, partner, out, back).start()

    def relayed(buffer, parts):
        await_all(recv_sem, parts[2], buffer.at[pl.ds(0, far)])

    spreads = [spread(kept.at[0])]
    for t in range(1, steps - 1):
        find_own(t)
    pick(1, steps - 1, True)
    for t in range(1, steps - 1):
        spreads.append(spread(kept.at[t]))

    for t in range(steps - 1):
        index_held[t] = window(support[t : t + 1, :], member(i) * width, width)
    find_own(steps - 1)

    def carried(t, value):
        diagonal = iota((KMAX, KMAX), 0) == iota((KMAX, KMAX), 1)
        after = jnp.sum(
            jnp.where(diagonal, index_held[t + 1].astype(F32), 0.0), axis=0, keepdims=True
        ).astype(jnp.int32)
        before = index_held[t]
        same = jnp.where(jnp.logical_and(before == after, before >= 0), 1.0, 0.0).astype(BF16)
        return add3(jnp.dot(split3(value), same, preferred_element_type=F32))

    pl.when(on_diagonal)(
        lambda: await_all(recv_sem, first_back, first_recv.at[pl.ds(0, rows - 1)])
    )
    pl.when(off_diagonal)(lambda: await_all(recv_sem, first_back, first_recv))
    current = STEP_SIZE * jnp.sum(first_recv[...].astype(F32), axis=0)

    own_measured = measured[pl.ds(pl.multiple_of(q * group, group), group), :]
    energy = [jnp.sum(own_measured * own_measured)]
    for t in range(steps - 1):
        if t > 0:
            relayed(kept.at[t], spreads[t])
            slope = lax.dot_general(
                residual.astype(BF16),
                kept[t].reshape(rows * KMAX, depth),
                NEAR,
                preferred_element_type=F32,
            ).astype(BF16)
            for k in range(rows):
                slope_send[t - 1, k] = slope[:, k * KMAX : (k + 1) * KMAX]
            out, back = next(sending), next(landing)
            for n, peer in enumerate(row_peers):
                remote(
                    slope_send.at[t - 1, peer[0]], slope_recv.at[t - 1, n], peer, out, back
                ).start()
            sent.append((out, slope_recv.at[t - 1]))
            carry = carried(t - 1, held[...])
            await_all(recv_sem, back, slope_recv.at[t - 1])
            gathered = slope_send[t - 1, i].astype(F32) + jnp.sum(
                slope_recv[t - 1].astype(F32), axis=0
            )
            current = carry + STEP_SIZE * gathered
        held[...] = current
        current_all[t, i] = current.astype(BF16)
        out, back = next(sending), next(landing)
        mine = current_all.at[t, i]
        for peer in row_peers:
            remote(mine, mine, peer, out, back).start()
        others = current_all.at[t, pl.ds(0, rows - 1)]
        sent.append((out, others))
        if t == steps - 2:
            moved_send[...] = current
            move = remote(moved_send, moved_recv, (q, member(i)), next(sending), next(landing))
            pl.when(off_diagonal)(move.start)

            @pl.when(on_diagonal)
            def _():
                moved_recv[...] = moved_send[...]

        if t != 1:
            following = t if t == 0 else None
            if following is not None:
                relay(kept.at[0], spreads[0])
                relayed(kept.at[0], spreads[0])
        elif steps > 3:
            relay(kept.at[2], spreads[2])
        await_all(recv_sem, back, others)
        signals = jnp.concatenate([current_all[t, k] for k in range(rows)], axis=1)
        seen_all[t, h] = jnp.dot(
            signals, kept[t].reshape(rows * KMAX, depth), preferred_element_type=F32
        ).astype(BF16)
        out, back = next(sending), next(landing)
        mine = seen_all.at[t, h]
        for peer in h_peers:
            remote(mine, mine, peer, out, back).start()
        others = seen_all.at[t, pl.ds(0, high - 1)]
        sent.append((out, others))
        if t == 0:
            relay(kept.at[1], spreads[1])
        await_all(recv_sem, back, others)
        residual = own_measured - jnp.sum(seen_all[t].astype(F32), axis=0)
        energy.append(jnp.sum(residual * residual))

    lanes = iota((16, depth), 1)
    values = jnp.zeros((16, depth), F32)
    for t in range(steps):
        values = jnp.where(lanes == t, energy[t], values)
    top = values.astype(BF16).astype(F32)
    mid = (values - top).astype(BF16).astype(F32)
    low = values - top - mid
    line = iota((16, depth), 0)
    values = jnp.where(line == 0, top, jnp.where(line == 1, mid, jnp.where(line == 2, low, 0.0)))
    residual_all[q] = jnp.concatenate([residual.astype(BF16), values.astype(BF16)], axis=0)
    parts = spread(residual_all)
    relay(residual_all, parts)
    relayed(residual_all, parts)

    all_signals = jnp.concatenate([residual_all[k, :group, :] for k in range(rows)], axis=0)
    first_by_x = list(range(along_x))
    z_out, x_out = next(sending), next(sending)
    arrive = [next(landing) for _ in range(chunks)]
    across_first = list(range(along_x, chunks))
    order = []
    for n in range(max(len(first_by_x), len(across_first))):
        order += across_first[n : n + 1] + first_by_x[n : n + 1]
    for c in order:
        part = jnp.dot(
            all_signals, a_block[:, c * chunk : (c + 1) * chunk], preferred_element_type=F32
        ).astype(BF16)
        if c < along_x:
            for k in range(rows):
                grad_send[c, k % pairs * 2 + k // pairs] = part[k * group : (k + 1) * group, :]
            for n, peer in enumerate(x_peers):
                remote(
                    grad_send.at[c, pl.ds(lax.rem(peer[0], pairs) * 2, 2)],
                    by_x.at[c, n],
                    peer,
                    x_out,
                    arrive[c],
                ).start()
        else:
            for k in range(rows):
                grad_send[c, k] = part[k * group : (k + 1) * group, :]
            remote(
                grad_send.at[c, pl.ds((1 - z) * pairs, pairs)],
                by_z.at[c - along_x],
                across,
                z_out,
                arrive[c],
            ).start()
    sent.append((x_out, by_x))
    sent.append((z_out, by_z))
    second = {}
    pair_out, line_out = next(sending), next(sending)
    for c in order:
        second[c] = next(landing)
        if c < along_x:
            await_all(recv_sem, arrive[c], by_x.at[c])
            total = grad_send[c, pl.ds(x * 2, 2)].astype(F32)
            for n in range(pairs - 1):
                total += by_x[c, n].astype(F32)
            pair_send[c] = total.astype(BF16)
            remote(
                pair_send.at[c, 1 - z], pair_recv.at[c], across, pair_out, second[c]
            ).start()
        else:
            n = c - along_x
            await_all(recv_sem, arrive[c], by_z.at[n])
            total = grad_send[c, pl.ds(z * pairs, pairs)].astype(F32) + by_z[n].astype(F32)
            line_send[n] = total.astype(BF16)
            for m, peer in enumerate(x_peers):
                remote(
                    line_send.at[n, lax.rem(peer[0], pairs)],
                    line_recv.at[n, m],
                    peer,
                    line_out,
                    second[c],
                ).start()
    sent.append((pair_out, pair_recv))
    sent.append((line_out, line_recv))

    norm_all[i, :, width:] = jnp.sum(
        jnp.sum(residual_all[:, group:, :KMAX].astype(F32), axis=0), axis=0, keepdims=True
    )
    pl.when(off_diagonal)(move.wait_recv)
    moved = split3(moved_recv[...])
    for c in order:
        span = slice(c * chunk, (c + 1) * chunk)
        before = add3(
            jnp.dot(
                moved,
                one_hot(index_own[steps - 2], c * chunk, chunk).astype(BF16),
                preferred_element_type=F32,
            )
        )
        mask = jnp.sum(one_hot(index_own[steps - 1], c * chunk, chunk), axis=0, keepdims=True)
        if c < along_x:
            await_all(recv_sem, second[c], pair_recv.at[c])
            gradient = pair_send[c, z].astype(F32) + pair_recv[c].astype(F32)
        else:
            n = c - along_x
            await_all(recv_sem, second[c], line_recv.at[n])
            gradient = line_send[n, x].astype(F32) + jnp.sum(line_recv[n].astype(F32), axis=0)
        stepped = before + STEP_SIZE * gradient
        kept_out[:, span] = stepped * mask
        norm_all[i, :, span] = jnp.sum(stepped * stepped, axis=0, keepdims=True)

    out, back = next(sending), next(landing)
    mine = norm_all.at[i]
    for peer in row_peers:
        remote(mine, mine, peer, out, back).start()
    others = norm_all.at[pl.ds(0, rows - 1)]
    sent.append((out, others))
    await_all(recv_sem, back, others)
    sums_out[...] = jnp.sum(norm_all[...], axis=0)

    pl.when(on_diagonal)(
        lambda: await_all(send_sem, first_out, first_send.at[pl.ds(0, rows - 1)])
    )
    pl.when(off_diagonal)(lambda: await_all(send_sem, first_out, first_send))
    pl.when(off_diagonal)(move.wait_send)
    for out, ref in sent:
        await_all(send_sem, out, ref)


def finish(total_count, kept, sums, estimate, norms, energies):
    width = kept.shape[1]
    estimate[...] = kept[...]
    norms[...] = jnp.sqrt(sums[:, :width]).reshape(width)
    for t in range(energies.shape[0]):
        energies[t] = sums[0, width + t] / total_count


def solution(mesh, far=4, high=4, chunk=512, along_x=4):
    rows = mesh.shape["row"]

    def local(matrix, measured, support):
        depth, width = matrix.shape
        signals = measured.shape[0]
        group = signals // rows
        pairs = rows // 2
        steps = support.shape[0]
        turns = steps - 1
        span = min(chunk, width)
        chunks = width // span
        along_z = chunks - along_x
        in_vmem = pl.BlockSpec(memory_space=pltpu.VMEM)
        in_hbm = pl.BlockSpec(memory_space=pltpu.HBM)
        kept, sums = pl.pallas_call(
            functools.partial(kernel, (rows, far, high, along_x)),
            out_shape=(
                jax.ShapeDtypeStruct((group, width), F32),
                jax.ShapeDtypeStruct((1, width + KMAX), F32),
            ),
            in_specs=[in_hbm] * 3,
            out_specs=(in_vmem,) * 2,
            scratch_shapes=[
                pltpu.VMEM(support.shape, jnp.int32),
                pltpu.VMEM(measured.shape, F32),
                pltpu.VMEM((depth, width), BF16),
                pltpu.VMEM((steps, KMAX, 1), jnp.int32),
                pltpu.VMEM((turns, KMAX, 1), jnp.int32),
                pltpu.VMEM((turns * KMAX, depth), F32),
                pltpu.VMEM((turns, rows, KMAX, depth), BF16),
                pltpu.VMEM((rows, group, KMAX), BF16),
                pltpu.VMEM((rows, group, KMAX), BF16),
                pltpu.VMEM((turns, rows, group, KMAX), BF16),
                pltpu.VMEM((turns, rows - 1, group, KMAX), BF16),
                pltpu.VMEM((turns, rows, group, KMAX), BF16),
                pltpu.VMEM((group, KMAX), F32),
                pltpu.VMEM((turns, high, group, depth), BF16),
                pltpu.VMEM((group, KMAX), F32),
                pltpu.VMEM((group, KMAX), F32),
                pltpu.VMEM((rows, group + 16, depth), BF16),
                pltpu.VMEM((chunks, rows, group, span), BF16),
                pltpu.VMEM((along_x, pairs - 1, 2, group, span), BF16),
                pltpu.VMEM((along_z, pairs, group, span), BF16),
                pltpu.VMEM((along_x, 2, group, span), BF16),
                pltpu.VMEM((along_x, group, span), BF16),
                pltpu.VMEM((along_z, pairs, group, span), BF16),
                pltpu.VMEM((along_z, pairs - 1, group, span), BF16),
                pltpu.VMEM((rows, 1, width + KMAX), F32),
                pltpu.SemaphoreType.DMA((chunks + 2,)),
                pltpu.SemaphoreType.DMA((19,)),
                pltpu.SemaphoreType.DMA((28 + 2 * chunks,)),
            ],
            compiler_params=pltpu.CompilerParams(
                collective_id=0, has_side_effects=True, vmem_limit_bytes=40 * 2**20
            ),
        )(*(pltpu.with_memory_space_constraint(a, pltpu.HBM) for a in (support, measured, matrix)))
        return pl.pallas_call(
            functools.partial(finish, float(signals * depth * rows)),
            out_shape=(
                jax.ShapeDtypeStruct((group, width), F32),
                jax.ShapeDtypeStruct((width,), F32),
                jax.ShapeDtypeStruct((steps,), F32),
            ),
            in_specs=[in_vmem] * 2,
            out_specs=(in_vmem, in_vmem, pl.BlockSpec(memory_space=pltpu.SMEM)),
            compiler_params=pltpu.CompilerParams(vmem_limit_bytes=4 * 2**20),
        )(kept, sums)

    return jax.shard_map(
        local,
        mesh=mesh,
        in_specs=(P("row", "col"), P(None, "row"), P()),
        out_specs=(P("row", "col"), P("col"), P()),
        check_vma=False,
    )
```

time: 105 us -> 87.9 us (0.84)
  the two profiles are of different devices: /device:TPU:32 before, /device:TPU:1 now
where the time goes in v2:
time: 87.9 us; the launch traced here: 87.8 us
  Pallas kernels  87.1 us (99%)
    pallas_call x1, Pallas kernels, local(): pl.pallas_call(functools.partial(kernel, (rows, far, high, along_x)), out...  86.3 us

profile of v2, /device:TPU:1, one launch (start us, length us, event | category | flops | bytes accessed | tf_op | source)
XLA Modules:
  0.0 87.8 jit_solution(16241116258042668326)
XLA Ops:
  0.6 86.3 %shard_map.58 = (f32[32,4096]{1,0:T(8,128)S(1)}, f32[1,4224]{1,0:T(1,128)S(1)}) custom-call(s32[4,2048]{1,0:T(4,128)} %support_in.1, f32[256,512]{1,0:T(8,128)} %measured_in.1, bf16[512,4096]{1,0:T(8,128)(2,1)} %matrix.1), custom_call_target="tpu_custom_call" | custom-call | tf_op jit(solution)/shard_map/pallas_call | solution.py:478
  86.9 0.8 shard_map.59

commit v3 on v2

--- a/solution.py
+++ b/solution.py
@@ -10,6 +10,7 @@
 KMAX = 128
 STEP_SIZE = 0.25
 CORES = 2
+LEAD = 1
 NEAR = (((1,), (1,)), ((), ()))
 F32 = jnp.float32
 BF16 = jnp.bfloat16
@@ -61,7 +62,6 @@
     a_block,
     index_own,
     index_held,
-    image,
     kept,
     first_send,
     first_recv,
@@ -73,6 +73,8 @@
     moved_send,
     moved_recv,
     residual_all,
+    energy_all,
+    energy_sum,
     grad_send,
     by_x,
     by_z,
@@ -89,6 +91,7 @@
     pairs = rows // 2
     depth, width = matrix.shape
     group = measured.shape[0] // rows
+    party = CORES * group
     steps = support.shape[0]
     chunk = grad_send.shape[3]
     chunks = width // chunk
@@ -100,9 +103,12 @@
     h = lax.rem(col // CORES, high)
     y = col // (CORES * high)
     q = y * CORES + core
+    lead = core == LEAD
+    follow = core != LEAD
     sending = iter(range(send_sem.shape[0]))
     landing = iter(range(recv_sem.shape[0]))
     sent = []
+    lead_sent = []
 
     def at(yy, hh, cc):
         return (yy * high + hh) * CORES + cc
@@ -134,31 +140,47 @@
     x_peers = [(z * pairs + lax.rem(x + d, pairs), col) for d in x_shift]
     across = ((1 - z) * pairs + x, col)
     y_shift = far_first(far)
-    y_peers = [(i, at(lax.rem(y + d, far), h, core)) for d in y_shift]
+    y_near = [lax.rem(y + d, far) for d in y_shift]
     y_from = [lax.rem(y - d + far, far) for d in y_shift]
+    y_leads = [(i, at(yy, h, LEAD)) for yy in y_near]
     h_peers = [(i, at(y, lax.rem(h + d, high), core)) for d in far_first(high)]
     partner = (i, at(y, h, 1 - core))
-
+    holder = (q, at(i // CORES, h, LEAD))
+
+    support_load = pltpu.make_async_copy(support_in, support, load_sem.at[chunks])
+    support_load.start()
     barrier = pltpu.get_barrier_semaphore()
-    for peer in row_peers + y_peers + h_peers + [partner]:
+
+    def greet(peer):
         pl.semaphore_signal(
             barrier, inc=1, device_id=peer, device_id_type=pl.DeviceIdType.MESH
         )
+
     on_diagonal = i == q
-    off_diagonal = jnp.logical_not(on_diagonal)
-    for k in range(rows):
-
-        @pl.when(jnp.logical_or(off_diagonal, i != k))
-        def _():
-            pl.semaphore_signal(
-                barrier,
-                inc=1,
-                device_id=(k, member(i)),
-                device_id_type=pl.DeviceIdType.MESH,
+    loop = jnp.logical_and(on_diagonal, lead)
+    no_loop = jnp.logical_not(loop)
+    pl.when(no_loop)(lambda: greet(holder))
+    for peer in row_peers + [partner]:
+        greet(peer)
+
+    @pl.when(lead)
+    def _():
+        for k in range(rows):
+            pl.when(jnp.logical_or(jnp.logical_not(on_diagonal), i != k))(
+                lambda k=k: greet((k, member(i)))
             )
-
-    support_load = pltpu.make_async_copy(support_in, support, load_sem.at[chunks])
-    support_load.start()
+        for yy in y_near:
+            for cc in range(CORES):
+                greet((i, at(yy, h, cc)))
+        for peer in h_peers:
+            greet(peer)
+
+    greetings = (
+        len(row_peers) + 1 + len(y_leads) + far
+        + jnp.where(lead, len(h_peers) + CORES, 0)
+        - jnp.where(loop, 2, 0)
+    )
+
     loads = [
         pltpu.make_async_copy(
             matrix.at[:, pl.ds(c * chunk, chunk)],
@@ -198,55 +220,38 @@
     first = lax.dot_general(
         measured[...].astype(BF16), kept[0, q], NEAR, preferred_element_type=F32
     ).astype(BF16)
-    for k in range(rows):
-        first_send[k] = first[k * group : (k + 1) * group, :]
-
-    pl.semaphore_wait(
-        barrier,
-        len(row_peers + y_peers + h_peers) + 1 + rows - jnp.where(on_diagonal, 1, 0),
-    )
+    for k in range(far):
+        first_send[k] = first[k * party : (k + 1) * party, :]
+
+    pl.semaphore_wait(barrier, greetings)
 
     first_out, first_back = next(sending), next(landing)
-    for k in range(rows):
+    for k in range(far):
         copy = remote(
-            first_send.at[k], first_recv.at[i], (q, member(k)), first_out, first_back
+            first_send.at[k], first_recv.at[i], (q, at(k, h, LEAD)), first_out, first_back
         )
-        other = jnp.logical_or(off_diagonal, q != k)
+        other = jnp.logical_or(no_loop, y != k)
         pl.when(other)(copy.start)
 
         @pl.when(jnp.logical_not(other))
         def _():
             first_recv[i] = first_send[k]
 
-    def spread(buffer):
-        own = buffer.at[q]
-        out, back = next(sending), next(landing)
-        to_y = [remote(own, own, peer, out, next(landing)) for peer in y_peers]
-        for copy in to_y:
-            copy.start()
-        remote(own, own, partner, out, back).start()
-        sent.append((out, buffer.at[pl.ds(0, rows - 1)]))
-        return to_y, out, back
-
-    def relay(buffer, parts):
-        to_y, out, back = parts
-        for n, copy in enumerate(to_y):
-            copy.wait_recv()
-            slot = buffer.at[y_from[n] * CORES + core]
-            remote(slot, slot, partner, out, back).start()
-
-    def relayed(buffer, parts):
-        await_all(recv_sem, parts[2], buffer.at[pl.ds(0, far)])
-
-    spreads = [spread(kept.at[0])]
+    kept_out_sem = [next(sending) for _ in range(steps - 1)]
+    kept_back = [next(landing) for _ in range(steps - 1)]
+
+    def spread(t):
+        own = kept.at[t, q]
+        for peer in y_leads:
+            remote(own, own, peer, kept_out_sem[t], kept_back[t]).start()
+        pl.when(follow)(remote(own, own, partner, kept_out_sem[t], kept_back[t]).start)
+
+    spread(0)
     for t in range(1, steps - 1):
         find_own(t)
     pick(1, steps - 1, True)
     for t in range(1, steps - 1):
-        spreads.append(spread(kept.at[t]))
-
-    for t in range(steps - 1):
-        index_held[t] = window(support[t : t + 1, :], member(i) * width, width)
+        spread(t)
     find_own(steps - 1)
 
     def carried(t, value):
@@ -258,93 +263,113 @@
         same = jnp.where(jnp.logical_and(before == after, before >= 0), 1.0, 0.0).astype(BF16)
         return add3(jnp.dot(split3(value), same, preferred_element_type=F32))
 
-    pl.when(on_diagonal)(
-        lambda: await_all(recv_sem, first_back, first_recv.at[pl.ds(0, rows - 1)])
+    move_out, move_back = next(sending), next(landing)
+    energy_out, energy_back, total_out, total_back = (
+        next(sending), next(landing), next(sending), next(landing)
     )
-    pl.when(off_diagonal)(lambda: await_all(recv_sem, first_back, first_recv))
-    current = STEP_SIZE * jnp.sum(first_recv[...].astype(F32), axis=0)
-
-    own_measured = measured[pl.ds(pl.multiple_of(q * group, group), group), :]
-    energy = [jnp.sum(own_measured * own_measured)]
-    for t in range(steps - 1):
-        if t > 0:
-            relayed(kept.at[t], spreads[t])
-            slope = lax.dot_general(
-                residual.astype(BF16),
-                kept[t].reshape(rows * KMAX, depth),
-                NEAR,
-                preferred_element_type=F32,
+    r_out, r_back, pass_out, pass_back = (
+        next(sending), [next(landing) for _ in y_leads], next(sending), next(landing)
+    )
+    moves = [
+        remote(moved_send.at[n], moved_recv, (CORES * y + n, member(i)), move_out, move_back)
+        for n in range(CORES)
+    ]
+    here = [jnp.logical_and(on_diagonal, core == n) for n in range(CORES)]
+
+    @pl.when(lead)
+    def _():
+        for t in range(steps - 1):
+            index_held[t] = window(support[t : t + 1, :], member(i) * width, width)
+        pl.when(on_diagonal)(
+            lambda: await_all(recv_sem, first_back, first_recv.at[pl.ds(0, rows - 1)])
+        )
+        pl.when(jnp.logical_not(on_diagonal))(lambda: await_all(recv_sem, first_back, first_recv))
+        current = STEP_SIZE * jnp.sum(first_recv[...].astype(F32), axis=0)
+
+        own_measured = measured[pl.ds(pl.multiple_of(y * party, party), party), :]
+        energy = [jnp.sum(own_measured * own_measured)]
+        for t in range(steps - 1):
+            if t > 0:
+                await_all(recv_sem, kept_back[t], kept.at[t, pl.ds(0, rows - 1)])
+                slope = lax.dot_general(
+                    residual.astype(BF16),
+                    kept[t].reshape(rows * KMAX, depth),
+                    NEAR,
+                    preferred_element_type=F32,
+                ).astype(BF16)
+                for k in range(rows):
+                    slope_send[t - 1, k] = slope[:, k * KMAX : (k + 1) * KMAX]
+                out, back = next(sending), next(landing)
+                for n, peer in enumerate(row_peers):
+                    remote(
+                        slope_send.at[t - 1, peer[0]], slope_recv.at[t - 1, n], peer, out, back
+                    ).start()
+                lead_sent.append((out, lambda t=t: slope_recv.at[t - 1]))
+                carry = carried(t - 1, held[...])
+                await_all(recv_sem, back, slope_recv.at[t - 1])
+                gathered = slope_send[t - 1, i].astype(F32) + jnp.sum(
+                    slope_recv[t - 1].astype(F32), axis=0
+                )
+                current = carry + STEP_SIZE * gathered
+            held[...] = current
+            current_all[t, i] = current.astype(BF16)
+            out, back = next(sending), next(landing)
+            mine = current_all.at[t, i]
+            for peer in row_peers:
+                remote(mine, mine, peer, out, back).start()
+            others = current_all.at[t, pl.ds(0, rows - 1)]
+            lead_sent.append((out, lambda t=t: current_all.at[t, pl.ds(0, rows - 1)]))
+            if t == steps - 2:
+                for n in range(CORES):
+                    moved_send[n] = current[n * group : (n + 1) * group, :]
+                    pl.when(jnp.logical_not(here[n]))(moves[n].start)
+
+                    @pl.when(here[n])
+                    def _():
+                        moved_recv[...] = moved_send[n]
+
+            if t == 0:
+                await_all(recv_sem, kept_back[t], kept.at[t, pl.ds(0, rows - 1)])
+            await_all(recv_sem, back, others)
+            signals = jnp.concatenate([current_all[t, k] for k in range(rows)], axis=1)
+            seen_all[t, h] = jnp.dot(
+                signals, kept[t].reshape(rows * KMAX, depth), preferred_element_type=F32
             ).astype(BF16)
-            for k in range(rows):
-                slope_send[t - 1, k] = slope[:, k * KMAX : (k + 1) * KMAX]
             out, back = next(sending), next(landing)
-            for n, peer in enumerate(row_peers):
-                remote(
-                    slope_send.at[t - 1, peer[0]], slope_recv.at[t - 1, n], peer, out, back
-                ).start()
-            sent.append((out, slope_recv.at[t - 1]))
-            carry = carried(t - 1, held[...])
-            await_all(recv_sem, back, slope_recv.at[t - 1])
-            gathered = slope_send[t - 1, i].astype(F32) + jnp.sum(
-                slope_recv[t - 1].astype(F32), axis=0
-            )
-            current = carry + STEP_SIZE * gathered
-        held[...] = current
-        current_all[t, i] = current.astype(BF16)
-        out, back = next(sending), next(landing)
-        mine = current_all.at[t, i]
-        for peer in row_peers:
-            remote(mine, mine, peer, out, back).start()
-        others = current_all.at[t, pl.ds(0, rows - 1)]
-        sent.append((out, others))
-        if t == steps - 2:
-            moved_send[...] = current
-            move = remote(moved_send, moved_recv, (q, member(i)), next(sending), next(landing))
-            pl.when(off_diagonal)(move.start)
-
-            @pl.when(on_diagonal)
-            def _():
-                moved_recv[...] = moved_send[...]
-
-        if t != 1:
-            following = t if t == 0 else None
-            if following is not None:
-                relay(kept.at[0], spreads[0])
-                relayed(kept.at[0], spreads[0])
-        elif steps > 3:
-            relay(kept.at[2], spreads[2])
-        await_all(recv_sem, back, others)
-        signals = jnp.concatenate([current_all[t, k] for k in range(rows)], axis=1)
-        seen_all[t, h] = jnp.dot(
-            signals, kept[t].reshape(rows * KMAX, depth), preferred_element_type=F32
-        ).astype(BF16)
-        out, back = next(sending), next(landing)
-        mine = seen_all.at[t, h]
-        for peer in h_peers:
-            remote(mine, mine, peer, out, back).start()
-        others = seen_all.at[t, pl.ds(0, high - 1)]
-        sent.append((out, others))
-        if t == 0:
-            relay(kept.at[1], spreads[1])
-        await_all(recv_sem, back, others)
-        residual = own_measured - jnp.sum(seen_all[t].astype(F32), axis=0)
-        energy.append(jnp.sum(residual * residual))
-
-    lanes = iota((16, depth), 1)
-    values = jnp.zeros((16, depth), F32)
-    for t in range(steps):
-        values = jnp.where(lanes == t, energy[t], values)
-    top = values.astype(BF16).astype(F32)
-    mid = (values - top).astype(BF16).astype(F32)
-    low = values - top - mid
-    line = iota((16, depth), 0)
-    values = jnp.where(line == 0, top, jnp.where(line == 1, mid, jnp.where(line == 2, low, 0.0)))
-    residual_all[q] = jnp.concatenate([residual.astype(BF16), values.astype(BF16)], axis=0)
-    parts = spread(residual_all)
-    relay(residual_all, parts)
-    relayed(residual_all, parts)
-
-    all_signals = jnp.concatenate([residual_all[k, :group, :] for k in range(rows)], axis=0)
+            mine = seen_all.at[t, h]
+            for peer in h_peers:
+                remote(mine, mine, peer, out, back).start()
+            others = seen_all.at[t, pl.ds(0, high - 1)]
+            lead_sent.append((out, lambda t=t: seen_all.at[t, pl.ds(0, high - 1)]))
+            await_all(recv_sem, back, others)
+            residual = own_measured - jnp.sum(seen_all[t].astype(F32), axis=0)
+            energy.append(jnp.sum(residual * residual))
+
+        residual_all[y] = residual.astype(BF16)
+        own = residual_all.at[y]
+        copies = [remote(own, own, peer, r_out, r_back[n]) for n, peer in enumerate(y_leads)]
+        for copy in copies:
+            copy.start()
+        remote(own, own, partner, pass_out, pass_back).start()
+        lanes = iota((1, KMAX), 1)
+        values = jnp.zeros((1, KMAX), F32)
+        for t in range(steps):
+            values = jnp.where(lanes == t, energy[t], values)
+        energy_all[y] = values
+        mine = energy_all.at[y]
+        for peer in y_leads:
+            remote(mine, mine, peer, energy_out, energy_back).start()
+        for n, copy in enumerate(copies):
+            copy.wait_recv()
+            slot = residual_all.at[y_from[n]]
+            remote(slot, slot, partner, pass_out, pass_back).start()
+        lead_sent.append((r_out, lambda: residual_all.at[pl.ds(0, far - 1)]))
+        lead_sent.append((pass_out, lambda: residual_all))
+        lead_sent.append((energy_out, lambda: energy_all.at[pl.ds(0, far - 1)]))
+
+    pl.when(follow)(lambda: await_all(recv_sem, pass_back, residual_all))
+
+    all_signals = jnp.concatenate([residual_all[k] for k in range(far)], axis=0)
     first_by_x = list(range(along_x))
     z_out, x_out = next(sending), next(sending)
     arrive = [next(landing) for _ in range(chunks)]
@@ -379,6 +404,14 @@
             ).start()
     sent.append((x_out, by_x))
     sent.append((z_out, by_z))
+
+    @pl.when(lead)
+    def _():
+        await_all(recv_sem, energy_back, energy_all.at[pl.ds(0, far - 1)])
+        energy_sum[...] = jnp.sum(energy_all[...], axis=0)
+        remote(energy_sum, energy_sum, partner, total_out, total_back).start()
+        lead_sent.append((total_out, lambda: energy_sum))
+
     second = {}
     pair_out, line_out = next(sending), next(sending)
     for c in order:
@@ -408,10 +441,9 @@
     sent.append((pair_out, pair_recv))
     sent.append((line_out, line_recv))
 
-    norm_all[i, :, width:] = jnp.sum(
-        jnp.sum(residual_all[:, group:, :KMAX].astype(F32), axis=0), axis=0, keepdims=True
-    )
-    pl.when(off_diagonal)(move.wait_recv)
+    pl.when(follow)(lambda: await_all(recv_sem, total_back, energy_sum))
+    norm_all[i, :, width:] = energy_sum[...]
+    pl.when(no_loop)(lambda: await_all(recv_sem, move_back, moved_recv))
     moved = split3(moved_recv[...])
     for c in order:
         span = slice(c * chunk, (c + 1) * chunk)
@@ -443,13 +475,26 @@
     await_all(recv_sem, back, others)
     sums_out[...] = jnp.sum(norm_all[...], axis=0)
 
-    pl.when(on_diagonal)(
-        lambda: await_all(send_sem, first_out, first_send.at[pl.ds(0, rows - 1)])
+    pl.when(loop)(
+        lambda: await_all(send_sem, first_out, first_send.at[pl.ds(0, far - 1)])
     )
-    pl.when(off_diagonal)(lambda: await_all(send_sem, first_out, first_send))
-    pl.when(off_diagonal)(move.wait_send)
+    pl.when(no_loop)(lambda: await_all(send_sem, first_out, first_send))
     for out, ref in sent:
         await_all(send_sem, out, ref)
+
+    @pl.when(lead)
+    def _():
+        for t in range(steps - 1):
+            await_all(send_sem, kept_out_sem[t], kept.at[t, pl.ds(0, far - 1)])
+        for n in range(CORES):
+            pl.when(jnp.logical_not(here[n]))(moves[n].wait_send)
+        for out, ref in lead_sent:
+            await_all(send_sem, out, ref())
+
+    @pl.when(follow)
+    def _():
+        for t in range(steps - 1):
+            await_all(send_sem, kept_out_sem[t], kept.at[t, pl.ds(0, far)])
 
 
 def finish(total_count, kept, sums, estimate, norms, energies):
@@ -460,13 +505,14 @@
         energies[t] = sums[0, width + t] / total_count
 
 
-def solution(mesh, far=4, high=4, chunk=512, along_x=4):
+def solution(mesh, far=4, high=4, chunk=512, along_x=3):
     rows = mesh.shape["row"]
 
     def local(matrix, measured, support):
         depth, width = matrix.shape
         signals = measured.shape[0]
         group = signals // rows
+        party = CORES * group
         pairs = rows // 2
         steps = support.shape[0]
         turns = steps - 1
@@ -489,18 +535,19 @@
                 pltpu.VMEM((depth, width), BF16),
                 pltpu.VMEM((steps, KMAX, 1), jnp.int32),
                 pltpu.VMEM((turns, KMAX, 1), jnp.int32),
-                pltpu.VMEM((turns * KMAX, depth), F32),
                 pltpu.VMEM((turns, rows, KMAX, depth), BF16),
-                pltpu.VMEM((rows, group, KMAX), BF16),
-                pltpu.VMEM((rows, group, KMAX), BF16),
-                pltpu.VMEM((turns, rows, group, KMAX), BF16),
-                pltpu.VMEM((turns, rows - 1, group, KMAX), BF16),
-                pltpu.VMEM((turns, rows, group, KMAX), BF16),
+                pltpu.VMEM((far, party, KMAX), BF16),
+                pltpu.VMEM((rows, party, KMAX), BF16),
+                pltpu.VMEM((turns, rows, party, KMAX), BF16),
+                pltpu.VMEM((turns, rows - 1, party, KMAX), BF16),
+                pltpu.VMEM((turns, rows, party, KMAX), BF16),
+                pltpu.VMEM((party, KMAX), F32),
+                pltpu.VMEM((turns, high, party, depth), BF16),
+                pltpu.VMEM((CORES, group, KMAX), F32),
                 pltpu.VMEM((group, KMAX), F32),
-                pltpu.VMEM((turns, high, group, depth), BF16),
-                pltpu.VMEM((group, KMAX), F32),
-                pltpu.VMEM((group, KMAX), F32),
-                pltpu.VMEM((rows, group + 16, depth), BF16),
+                pltpu.VMEM((far, party, depth), BF16),
+                pltpu.VMEM((far, 1, KMAX), F32),
+                pltpu.VMEM((1, KMAX), F32),
                 pltpu.VMEM((chunks, rows, group, span), BF16),
                 pltpu.VMEM((along_x, pairs - 1, 2, group, span), BF16),
                 pltpu.VMEM((along_z, pairs, group, span), BF16),
@@ -510,8 +557,8 @@
                 pltpu.VMEM((along_z, pairs - 1, group, span), BF16),
                 pltpu.VMEM((rows, 1, width + KMAX), F32),
                 pltpu.SemaphoreType.DMA((chunks + 2,)),
-                pltpu.SemaphoreType.DMA((19,)),
-                pltpu.SemaphoreType.DMA((28 + 2 * chunks,)),
+                pltpu.SemaphoreType.DMA((22,)),
+                pltpu.SemaphoreType.DMA((20 + 2 * chunks,)),
             ],
             compiler_params=pltpu.CompilerParams(
                 collective_id=0, has_side_effects=True, vmem_limit_bytes=40 * 2**20

time: 87.9 us -> 83.8 us (0.953)
  the two profiles are of different devices: /device:TPU:1 before, /device:TPU:32 now
where the time goes in v3:
time: 83.8 us; the launch traced here: 83.7 us
  Pallas kernels  83.1 us (99%)
    pallas_call x1, Pallas kernels, local(): pl.pallas_call(functools.partial(kernel, (rows, far, high, along_x)), out...  82.2 us

profile of v3, /device:TPU:32, one launch (start us, length us, event | category | flops | bytes accessed | tf_op | source)
XLA Modules:
  0.0 83.7 jit_solution(9499575696625986289)
XLA Ops:
  0.6 82.2 %shard_map.58 = (f32[32,4096]{1,0:T(8,128)S(1)}, f32[1,4224]{1,0:T(1,128)S(1)}) custom-call(s32[4,2048]{1,0:T(4,128)} %support_in.1, f32[256,512]{1,0:T(8,128)} %measured_in.1, bf16[512,4096]{1,0:T(8,128)(2,1)} %matrix.1), custom_call_target="tpu_custom_call" | custom-call | tf_op jit(solution)/shard_map/pallas_call | solution.py:524
  82.9 0.8 %shard_map.59 = (f32[32,4096]{1,0:T(8,128)}, f32[4096]{0:T(1024)}, f32[4]{0:T(128)}) custom-call(f32[32,4096]{1,0:T(8,128)S(1)} %get-tuple-element.5.kept, f32[1,4224]{1,0:T(1,128)S(1)} %get-tuple-element.6.sums), custom_call_target="tpu_custom_call" | custom-call | tf_op jit(solution)/shard_map/pallas_call | solution.py:567

commit v4 on v3

--- a/solution.py
+++ b/solution.py
@@ -75,9 +75,14 @@
     residual_all,
     energy_all,
     energy_sum,
-    grad_send,
-    by_x,
-    by_z,
+    near_x,
+    near_z,
+    near_by_x,
+    near_by_z,
+    rest_x,
+    rest_z,
+    rest_by_x,
+    rest_by_z,
     pair_send,
     pair_recv,
     line_send,
@@ -91,9 +96,10 @@
     pairs = rows // 2
     depth, width = matrix.shape
     group = measured.shape[0] // rows
-    party = CORES * group
+    part = group // far
+    party = rows * part
     steps = support.shape[0]
-    chunk = grad_send.shape[3]
+    chunk = near_x.shape[3]
     chunks = width // chunk
     i = lax.axis_index("row")
     col = lax.axis_index("col")
@@ -145,42 +151,11 @@
     y_leads = [(i, at(yy, h, LEAD)) for yy in y_near]
     h_peers = [(i, at(y, lax.rem(h + d, high), core)) for d in far_first(high)]
     partner = (i, at(y, h, 1 - core))
-    holder = (q, at(i // CORES, h, LEAD))
+    def rows_of(k, yy):
+        return pl.ds(pl.multiple_of(k * group + yy * part, part), part)
 
     support_load = pltpu.make_async_copy(support_in, support, load_sem.at[chunks])
     support_load.start()
-    barrier = pltpu.get_barrier_semaphore()
-
-    def greet(peer):
-        pl.semaphore_signal(
-            barrier, inc=1, device_id=peer, device_id_type=pl.DeviceIdType.MESH
-        )
-
-    on_diagonal = i == q
-    loop = jnp.logical_and(on_diagonal, lead)
-    no_loop = jnp.logical_not(loop)
-    pl.when(no_loop)(lambda: greet(holder))
-    for peer in row_peers + [partner]:
-        greet(peer)
-
-    @pl.when(lead)
-    def _():
-        for k in range(rows):
-            pl.when(jnp.logical_or(jnp.logical_not(on_diagonal), i != k))(
-                lambda k=k: greet((k, member(i)))
-            )
-        for yy in y_near:
-            for cc in range(CORES):
-                greet((i, at(yy, h, cc)))
-        for peer in h_peers:
-            greet(peer)
-
-    greetings = (
-        len(row_peers) + 1 + len(y_leads) + far
-        + jnp.where(lead, len(h_peers) + CORES, 0)
-        - jnp.where(loop, 2, 0)
-    )
-
     loads = [
         pltpu.make_async_copy(
             matrix.at[:, pl.ds(c * chunk, chunk)],
@@ -193,6 +168,39 @@
         load.start()
     measured_load = pltpu.make_async_copy(measured_in, measured, load_sem.at[chunks + 1])
     measured_load.start()
+    barrier = pltpu.get_barrier_semaphore()
+
+    def greet(peer):
+        pl.semaphore_signal(
+            barrier, inc=1, device_id=peer, device_id_type=pl.DeviceIdType.MESH
+        )
+
+    on_diagonal = i == q
+    loop = jnp.logical_and(on_diagonal, lead)
+    no_loop = jnp.logical_not(loop)
+    for k in range(far):
+        pl.when(jnp.logical_or(no_loop, y != k))(lambda k=k: greet((q, at(k, h, LEAD))))
+    for peer in row_peers + [partner]:
+        greet(peer)
+
+    @pl.when(lead)
+    def _():
+        for k in range(rows):
+            pl.when(jnp.logical_or(jnp.logical_not(on_diagonal), i != k))(
+                lambda k=k: greet((k, member(i)))
+            )
+        for yy in y_near:
+            for cc in range(CORES):
+                greet((i, at(yy, h, cc)))
+        for peer in h_peers:
+            greet(peer)
+
+    greetings = (
+        len(row_peers) + 1 + len(y_leads) + far
+        + jnp.where(lead, len(h_peers) + rows, 0)
+        - jnp.where(loop, 2, 0)
+    )
+
     support_load.wait()
 
     def find_own(t):
@@ -219,9 +227,11 @@
 
     first = lax.dot_general(
         measured[...].astype(BF16), kept[0, q], NEAR, preferred_element_type=F32
-    ).astype(BF16)
-    for k in range(far):
-        first_send[k] = first[k * party : (k + 1) * party, :]
+    )
+    for n in range(far):
+        first_send[n] = jnp.concatenate(
+            [first[k * group + n * part :][:part] for k in range(rows)], axis=0
+        ).astype(BF16)
 
     pl.semaphore_wait(barrier, greetings)
 
@@ -267,14 +277,13 @@
     energy_out, energy_back, total_out, total_back = (
         next(sending), next(landing), next(sending), next(landing)
     )
-    r_out, r_back, pass_out, pass_back = (
-        next(sending), [next(landing) for _ in y_leads], next(sending), next(landing)
-    )
+    r_out, r_back = next(sending), [next(landing) for _ in y_leads]
+    pass_out, own_back, pass_back = next(sending), next(landing), next(landing)
     moves = [
-        remote(moved_send.at[n], moved_recv, (CORES * y + n, member(i)), move_out, move_back)
-        for n in range(CORES)
+        remote(moved_send.at[k], moved_recv.at[y], (k, member(i)), move_out, move_back)
+        for k in range(rows)
     ]
-    here = [jnp.logical_and(on_diagonal, core == n) for n in range(CORES)]
+    here = [jnp.logical_and(on_diagonal, i == k) for k in range(rows)]
 
     @pl.when(lead)
     def _():
@@ -286,7 +295,9 @@
         pl.when(jnp.logical_not(on_diagonal))(lambda: await_all(recv_sem, first_back, first_recv))
         current = STEP_SIZE * jnp.sum(first_recv[...].astype(F32), axis=0)
 
-        own_measured = measured[pl.ds(pl.multiple_of(y * party, party), party), :]
+        own_measured = jnp.concatenate(
+            [measured[rows_of(k, y), :] for k in range(rows)], axis=0
+        )
         energy = [jnp.sum(own_measured * own_measured)]
         for t in range(steps - 1):
             if t > 0:
@@ -320,13 +331,13 @@
             others = current_all.at[t, pl.ds(0, rows - 1)]
             lead_sent.append((out, lambda t=t: current_all.at[t, pl.ds(0, rows - 1)]))
             if t == steps - 2:
-                for n in range(CORES):
-                    moved_send[n] = current[n * group : (n + 1) * group, :]
-                    pl.when(jnp.logical_not(here[n]))(moves[n].start)
-
-                    @pl.when(here[n])
+                for k in range(rows):
+                    moved_send[k] = current[k * part : (k + 1) * part, :]
+                    pl.when(jnp.logical_not(here[k]))(moves[k].start)
+
+                    @pl.when(here[k])
                     def _():
-                        moved_recv[...] = moved_send[n]
+                        moved_recv[y] = moved_send[k]
 
             if t == 0:
                 await_all(recv_sem, kept_back[t], kept.at[t, pl.ds(0, rows - 1)])
@@ -347,10 +358,9 @@
 
         residual_all[y] = residual.astype(BF16)
         own = residual_all.at[y]
-        copies = [remote(own, own, peer, r_out, r_back[n]) for n, peer in enumerate(y_leads)]
-        for copy in copies:
-            copy.start()
-        remote(own, own, partner, pass_out, pass_back).start()
+        for n, peer in enumerate(y_leads):
+            remote(own, own, peer, r_out, r_back[n]).start()
+        remote(own, own, partner, pass_out, own_back).start()
         lanes = iota((1, KMAX), 1)
         values = jnp.zeros((1, KMAX), F32)
         for t in range(steps):
@@ -359,51 +369,66 @@
         mine = energy_all.at[y]
         for peer in y_leads:
             remote(mine, mine, peer, energy_out, energy_back).start()
-        for n, copy in enumerate(copies):
-            copy.wait_recv()
-            slot = residual_all.at[y_from[n]]
-            remote(slot, slot, partner, pass_out, pass_back).start()
         lead_sent.append((r_out, lambda: residual_all.at[pl.ds(0, far - 1)]))
         lead_sent.append((pass_out, lambda: residual_all))
         lead_sent.append((energy_out, lambda: energy_all.at[pl.ds(0, far - 1)]))
 
-    pl.when(follow)(lambda: await_all(recv_sem, pass_back, residual_all))
-
-    all_signals = jnp.concatenate([residual_all[k] for k in range(far)], axis=0)
+    pl.when(follow)(lambda: await_all(recv_sem, own_back, residual_all.at[0]))
+
+    z_out, x_out, near_z_out, near_x_out = (next(sending) for _ in range(4))
+    near_back = [next(landing) for _ in range(chunks)]
+    rest_back = [next(landing) for _ in range(chunks)]
     first_by_x = list(range(along_x))
-    z_out, x_out = next(sending), next(sending)
-    arrive = [next(landing) for _ in range(chunks)]
     across_first = list(range(along_x, chunks))
     order = []
     for n in range(max(len(first_by_x), len(across_first))):
         order += across_first[n : n + 1] + first_by_x[n : n + 1]
-    for c in order:
-        part = jnp.dot(
-            all_signals, a_block[:, c * chunk : (c + 1) * chunk], preferred_element_type=F32
-        ).astype(BF16)
-        if c < along_x:
-            for k in range(rows):
-                grad_send[c, k % pairs * 2 + k // pairs] = part[k * group : (k + 1) * group, :]
-            for n, peer in enumerate(x_peers):
-                remote(
-                    grad_send.at[c, pl.ds(lax.rem(peer[0], pairs) * 2, 2)],
-                    by_x.at[c, n],
-                    peer,
-                    x_out,
-                    arrive[c],
-                ).start()
-        else:
-            for k in range(rows):
-                grad_send[c, k] = part[k * group : (k + 1) * group, :]
-            remote(
-                grad_send.at[c, pl.ds((1 - z) * pairs, pairs)],
-                by_z.at[c - along_x],
-                across,
-                z_out,
-                arrive[c],
-            ).start()
-    sent.append((x_out, by_x))
-    sent.append((z_out, by_z))
+
+    def send_dense(lhs, to_x, to_z, from_x, from_z, out_x, out_z, back):
+        count = lhs.shape[0] // party
+
+        def tile(product, k):
+            return [product[n * party + k * part :][:part] for n in range(count)]
+
+        for c in order:
+            product = jnp.dot(
+                lhs, a_block[:, c * chunk : (c + 1) * chunk], preferred_element_type=F32
+            )
+            if c < along_x:
+                for k in range(pairs):
+                    to_x[c, k] = jnp.concatenate(
+                        tile(product, k) + tile(product, pairs + k), axis=0
+                    ).astype(BF16)
+                for n, peer in enumerate(x_peers):
+                    remote(
+                        to_x.at[c, lax.rem(peer[0], pairs)], from_x.at[c, n], peer, out_x, back[c]
+                    ).start()
+            else:
+                n = c - along_x
+                for k in range(2):
+                    to_z[n, k] = jnp.concatenate(
+                        sum([tile(product, k * pairs + m) for m in range(pairs)], []), axis=0
+                    ).astype(BF16)
+                remote(to_z.at[n, 1 - z], from_z.at[n], across, out_z, back[c]).start()
+        sent.append((out_x, from_x))
+        sent.append((out_z, from_z))
+
+    send_dense(
+        residual_all[y], near_x, near_z, near_by_x, near_by_z, near_x_out, near_z_out, near_back
+    )
+
+    @pl.when(lead)
+    def _():
+        for n, yy in enumerate(y_from):
+            slot = residual_all.at[yy]
+            await_all(recv_sem, r_back[n], slot)
+            remote(slot, slot, partner, pass_out, pass_back).start()
+
+    pl.when(follow)(lambda: await_all(recv_sem, pass_back, residual_all.at[pl.ds(0, far - 1)]))
+    send_dense(
+        jnp.concatenate([residual_all[yy] for yy in y_from], axis=0),
+        rest_x, rest_z, rest_by_x, rest_by_z, x_out, z_out, rest_back,
+    )
 
     @pl.when(lead)
     def _():
@@ -412,24 +437,33 @@
         remote(energy_sum, energy_sum, partner, total_out, total_back).start()
         lead_sent.append((total_out, lambda: energy_sum))
 
+    rest = part * (far - 1)
     second = {}
     pair_out, line_out = next(sending), next(sending)
     for c in order:
         second[c] = next(landing)
         if c < along_x:
-            await_all(recv_sem, arrive[c], by_x.at[c])
-            total = grad_send[c, pl.ds(x * 2, 2)].astype(F32)
-            for n in range(pairs - 1):
-                total += by_x[c, n].astype(F32)
-            pair_send[c] = total.astype(BF16)
+            await_all(recv_sem, near_back[c], near_by_x.at[c])
+            near = near_x[c, x].astype(F32) + jnp.sum(near_by_x[c].astype(F32), axis=0)
+            await_all(recv_sem, rest_back[c], rest_by_x.at[c])
+            total = rest_x[c, x].astype(F32) + jnp.sum(rest_by_x[c].astype(F32), axis=0)
+            for k in range(2):
+                pair_send[c, k] = jnp.concatenate(
+                    [near[k * part :][:part], total[k * rest :][:rest]], axis=0
+                ).astype(BF16)
             remote(
                 pair_send.at[c, 1 - z], pair_recv.at[c], across, pair_out, second[c]
             ).start()
         else:
             n = c - along_x
-            await_all(recv_sem, arrive[c], by_z.at[n])
-            total = grad_send[c, pl.ds(z * pairs, pairs)].astype(F32) + by_z[n].astype(F32)
-            line_send[n] = total.astype(BF16)
+            await_all(recv_sem, near_back[c], near_by_z.at[n])
+            near = near_z[n, z].astype(F32) + near_by_z[n].astype(F32)
+            await_all(recv_sem, rest_back[c], rest_by_z.at[n])
+            total = rest_z[n, z].astype(F32) + rest_by_z[n].astype(F32)
+            for k in range(pairs):
+                line_send[n, k] = jnp.concatenate(
+                    [near[k * part :][:part], total[k * rest :][:rest]], axis=0
+                ).astype(BF16)
             for m, peer in enumerate(x_peers):
                 remote(
                     line_send.at[n, lax.rem(peer[0], pairs)],
@@ -443,8 +477,10 @@
 
     pl.when(follow)(lambda: await_all(recv_sem, total_back, energy_sum))
     norm_all[i, :, width:] = energy_sum[...]
+    pl.when(loop)(lambda: await_all(recv_sem, move_back, moved_recv.at[pl.ds(0, far - 1)]))
     pl.when(no_loop)(lambda: await_all(recv_sem, move_back, moved_recv))
-    moved = split3(moved_recv[...])
+    y_order = [y] + y_from
+    moved = split3(jnp.concatenate([moved_recv[yy] for yy in y_order], axis=0))
     for c in order:
         span = slice(c * chunk, (c + 1) * chunk)
         before = add3(
@@ -463,7 +499,9 @@
             await_all(recv_sem, second[c], line_recv.at[n])
             gradient = line_send[n, x].astype(F32) + jnp.sum(line_recv[n].astype(F32), axis=0)
         stepped = before + STEP_SIZE * gradient
-        kept_out[:, span] = stepped * mask
+        settled = stepped * mask
+        for n, yy in enumerate(y_order):
+            kept_out[rows_of(0, yy), span] = settled[n * part : (n + 1) * part]
         norm_all[i, :, span] = jnp.sum(stepped * stepped, axis=0, keepdims=True)
 
     out, back = next(sending), next(landing)
@@ -486,8 +524,8 @@
     def _():
         for t in range(steps - 1):
             await_all(send_sem, kept_out_sem[t], kept.at[t, pl.ds(0, far - 1)])
-        for n in range(CORES):
-            pl.when(jnp.logical_not(here[n]))(moves[n].wait_send)
+        for k in range(rows):
+            pl.when(jnp.logical_not(here[k]))(moves[k].wait_send)
         for out, ref in lead_sent:
             await_all(send_sem, out, ref())
 
@@ -512,7 +550,9 @@
         depth, width = matrix.shape
         signals = measured.shape[0]
         group = signals // rows
-        party = CORES * group
+        part = group // far
+        party = rows * part
+        rest = part * (far - 1)
         pairs = rows // 2
         steps = support.shape[0]
         turns = steps - 1
@@ -543,22 +583,27 @@
                 pltpu.VMEM((turns, rows, party, KMAX), BF16),
                 pltpu.VMEM((party, KMAX), F32),
                 pltpu.VMEM((turns, high, party, depth), BF16),
-                pltpu.VMEM((CORES, group, KMAX), F32),
-                pltpu.VMEM((group, KMAX), F32),
+                pltpu.VMEM((rows, part, KMAX), F32),
+                pltpu.VMEM((far, part, KMAX), F32),
                 pltpu.VMEM((far, party, depth), BF16),
                 pltpu.VMEM((far, 1, KMAX), F32),
                 pltpu.VMEM((1, KMAX), F32),
-                pltpu.VMEM((chunks, rows, group, span), BF16),
-                pltpu.VMEM((along_x, pairs - 1, 2, group, span), BF16),
-                pltpu.VMEM((along_z, pairs, group, span), BF16),
+                pltpu.VMEM((along_x, pairs, 2 * part, span), BF16),
+                pltpu.VMEM((along_z, 2, pairs * part, span), BF16),
+                pltpu.VMEM((along_x, pairs - 1, 2 * part, span), BF16),
+                pltpu.VMEM((along_z, pairs * part, span), BF16),
+                pltpu.VMEM((along_x, pairs, 2 * rest, span), BF16),
+                pltpu.VMEM((along_z, 2, pairs * rest, span), BF16),
+                pltpu.VMEM((along_x, pairs - 1, 2 * rest, span), BF16),
+                pltpu.VMEM((along_z, pairs * rest, span), BF16),
                 pltpu.VMEM((along_x, 2, group, span), BF16),
                 pltpu.VMEM((along_x, group, span), BF16),
                 pltpu.VMEM((along_z, pairs, group, span), BF16),
                 pltpu.VMEM((along_z, pairs - 1, group, span), BF16),
                 pltpu.VMEM((rows, 1, width + KMAX), F32),
                 pltpu.SemaphoreType.DMA((chunks + 2,)),
-                pltpu.SemaphoreType.DMA((22,)),
-                pltpu.SemaphoreType.DMA((20 + 2 * chunks,)),
+                pltpu.SemaphoreType.DMA((24,)),
+                pltpu.SemaphoreType.DMA((21 + 3 * chunks,)),
             ],
             compiler_params=pltpu.CompilerParams(
                 collective_id=0, has_side_effects=True, vmem_limit_bytes=40 * 2**20

time: 83.8 us -> 80.7 us (0.963)
  Pallas kernels: 83.1 us -> 80 us
    pallas_call x1, Pallas kernels: 82.2 us -> 79.1 us  [local(): pl.pallas_call(functools.partial(kernel, (rows, far, high, along_x)), out...]
where the time goes in v4:
time: 80.7 us; the launch traced here: 80.6 us
  Pallas kernels  80 us (99%)
    pallas_call x1, Pallas kernels, local(): pl.pallas_call(functools.partial(kernel, (rows, far, high, along_x)), out...  79.1 us

profile of v4, /device:TPU:32, one launch (start us, length us, event | category | flops | bytes accessed | tf_op | source)
XLA Modules:
  0.0 80.6 jit_solution(7058885039067295386)
XLA Ops:
  0.6 79.1 %shard_map.58 = (f32[32,4096]{1,0:T(8,128)S(1)}, f32[1,4224]{1,0:T(1,128)S(1)}) custom-call(s32[4,2048]{1,0:T(4,128)} %support_in.1, f32[256,512]{1,0:T(8,128)} %measured_in.1, bf16[512,4096]{1,0:T(8,128)(2,1)} %matrix.1), custom_call_target="tpu_custom_call" | custom-call | tf_op jit(solution)/shard_map/pallas_call | solution.py:564
  79.8 0.8 %shard_map.59 = (f32[32,4096]{1,0:T(8,128)}, f32[4096]{0:T(1024)}, f32[4]{0:T(128)}) custom-call(f32[32,4096]{1,0:T(8,128)S(1)} %get-tuple-element.5.kept, f32[1,4224]{1,0:T(1,128)S(1)} %get-tuple-element.6.sums), custom_call_target="tpu_custom_call" | custom-call | tf_op jit(solution)/shard_map/pallas_call | solution.py:612

commit v5 on v4

--- a/solution.py
+++ b/solution.py
@@ -178,6 +178,16 @@
     on_diagonal = i == q
     loop = jnp.logical_and(on_diagonal, lead)
     no_loop = jnp.logical_not(loop)
+
+    @pl.when(lead)
+    def _():
+        for k in range(rows):
+            pl.when(jnp.logical_or(jnp.logical_not(on_diagonal), i != k))(
+                lambda k=k: greet((k, member(i)))
+            )
+        for peer in h_peers:
+            greet(peer)
+
     for k in range(far):
         pl.when(jnp.logical_or(no_loop, y != k))(lambda k=k: greet((q, at(k, h, LEAD))))
     for peer in row_peers + [partner]:
@@ -185,15 +195,9 @@
 
     @pl.when(lead)
     def _():
-        for k in range(rows):
-            pl.when(jnp.logical_or(jnp.logical_not(on_diagonal), i != k))(
-                lambda k=k: greet((k, member(i)))
-            )
         for yy in y_near:
             for cc in range(CORES):
                 greet((i, at(yy, h, cc)))
-        for peer in h_peers:
-            greet(peer)
 
     greetings = (
         len(row_peers) + 1 + len(y_leads) + far
@@ -254,15 +258,20 @@
         own = kept.at[t, q]
         for peer in y_leads:
             remote(own, own, peer, kept_out_sem[t], kept_back[t]).start()
-        pl.when(follow)(remote(own, own, partner, kept_out_sem[t], kept_back[t]).start)
+        pl.when(follow)(lambda: remote(own, own, partner, kept_out_sem[t], kept_back[t]).start())
 
     spread(0)
     for t in range(1, steps - 1):
         find_own(t)
     pick(1, steps - 1, True)
-    for t in range(1, steps - 1):
-        spread(t)
     find_own(steps - 1)
+
+    @pl.when(follow)
+    def _():
+        for t in range(1, steps - 1):
+            await_all(send_sem, kept_out_sem[t - 1], kept.at[t - 1, pl.ds(0, far)])
+            spread(t)
+
 
     def carried(t, value):
         diagonal = iota((KMAX, KMAX), 0) == iota((KMAX, KMAX), 1)
@@ -339,6 +348,8 @@
                     def _():
                         moved_recv[y] = moved_send[k]
 
+            if t < steps - 2:
+                spread(t + 1)
             if t == 0:
                 await_all(recv_sem, kept_back[t], kept.at[t, pl.ds(0, rows - 1)])
             await_all(recv_sem, back, others)
@@ -382,10 +393,20 @@
     across_first = list(range(along_x, chunks))
     order = []
     for n in range(max(len(first_by_x), len(across_first))):
-        order += across_first[n : n + 1] + first_by_x[n : n + 1]
+        order += first_by_x[n : n + 1] + across_first[n : n + 1]
 
     def send_dense(lhs, to_x, to_z, from_x, from_z, out_x, out_z, back):
         count = lhs.shape[0] // party
+
+        def launch(c):
+            if c < along_x:
+                for n, peer in enumerate(x_peers):
+                    remote(
+                        to_x.at[c, lax.rem(peer[0], pairs)], from_x.at[c, n], peer, out_x, back[c]
+                    ).start()
+            else:
+                n = c - along_x
+                remote(to_z.at[n, 1 - z], from_z.at[n], across, out_z, back[c]).start()
 
         def tile(product, k):
             return [product[n * party + k * part :][:part] for n in range(count)]
@@ -399,17 +420,13 @@
                     to_x[c, k] = jnp.concatenate(
                         tile(product, k) + tile(product, pairs + k), axis=0
                     ).astype(BF16)
-                for n, peer in enumerate(x_peers):
-                    remote(
-                        to_x.at[c, lax.rem(peer[0], pairs)], from_x.at[c, n], peer, out_x, back[c]
-                    ).start()
             else:
                 n = c - along_x
                 for k in range(2):
                     to_z[n, k] = jnp.concatenate(
                         sum([tile(product, k * pairs + m) for m in range(pairs)], []), axis=0
                     ).astype(BF16)
-                remote(to_z.at[n, 1 - z], from_z.at[n], across, out_z, back[c]).start()
+            launch(c)
         sent.append((out_x, from_x))
         sent.append((out_z, from_z))
 
@@ -427,7 +444,13 @@
     pl.when(follow)(lambda: await_all(recv_sem, pass_back, residual_all.at[pl.ds(0, far - 1)]))
     send_dense(
         jnp.concatenate([residual_all[yy] for yy in y_from], axis=0),
-        rest_x, rest_z, rest_by_x, rest_by_z, x_out, z_out, rest_back,
+        rest_x,
+        rest_z,
+        rest_by_x,
+        rest_by_z,
+        x_out,
+        z_out,
+        rest_back,
     )
 
     @pl.when(lead)
@@ -531,8 +554,7 @@
 
     @pl.when(follow)
     def _():
-        for t in range(steps - 1):
-            await_all(send_sem, kept_out_sem[t], kept.at[t, pl.ds(0, far)])
+        await_all(send_sem, kept_out_sem[steps - 2], kept.at[steps - 2, pl.ds(0, far)])
 
 
 def finish(total_count, kept, sums, estimate, norms, energies):
@@ -543,7 +565,7 @@
         energies[t] = sums[0, width + t] / total_count
 
 
-def solution(mesh, far=4, high=4, chunk=512, along_x=3):
+def solution(mesh, far=4, high=4, chunk=512, along_x=4):
     rows = mesh.shape["row"]
 
     def local(matrix, measured, support):

time: 80.7 us -> 78.8 us (0.976)
  Pallas kernels: 80 us -> 78.1 us
    pallas_call x1, Pallas kernels: 79.1 us -> 77.3 us  [local(): pl.pallas_call(functools.partial(kernel, (rows, far, high, along_x)), out...]
where the time goes in v5:
time: 78.8 us
  Pallas kernels  78.1 us (99%)
    pallas_call x1, Pallas kernels, local(): pl.pallas_call(functools.partial(kernel, (rows, far, high, along_x)), out...  77.3 us

profile of v5, /device:TPU:32, one launch (start us, length us, event | category | flops | bytes accessed | tf_op | source)
XLA Modules:
  0.0 78.8 jit_solution(16010085416583347249)
XLA Ops:
  0.6 77.3 %shard_map.58 = (f32[32,4096]{1,0:T(8,128)S(1)}, f32[1,4224]{1,0:T(1,128)S(1)}) custom-call(s32[4,2048]{1,0:T(4,128)} %support_in.1, f32[256,512]{1,0:T(8,128)} %measured_in.1, bf16[512,4096]{1,0:T(8,128)(2,1)} %matrix.1), custom_call_target="tpu_custom_call" | custom-call | tf_op jit(solution)/shard_map/pallas_call | solution.py:586
  77.9 0.8 %shard_map.59 = (f32[32,4096]{1,0:T(8,128)}, f32[4096]{0:T(1024)}, f32[4]{0:T(128)}) custom-call(f32[32,4096]{1,0:T(8,128)S(1)} %get-tuple-element.5.kept, f32[1,4224]{1,0:T(1,128)S(1)} %get-tuple-element.6.sums), custom_call_target="tpu_custom_call" | custom-call | tf_op jit(solution)/shard_map/pallas_call | solution.py:634

commit v6 on v5

--- a/solution.py
+++ b/solution.py
@@ -63,6 +63,7 @@
     index_own,
     index_held,
     kept,
+    turned,
     first_send,
     first_recv,
     slope_send,
@@ -87,6 +88,8 @@
     pair_recv,
     line_send,
     line_recv,
+    carry_all,
+    mask_all,
     norm_all,
     load_sem,
     send_sem,
@@ -307,15 +310,11 @@
         own_measured = jnp.concatenate(
             [measured[rows_of(k, y), :] for k in range(rows)], axis=0
         )
-        energy = [jnp.sum(own_measured * own_measured)]
+        energy = [jnp.sum(own_measured * own_measured, axis=0, keepdims=True)]
         for t in range(steps - 1):
             if t > 0:
-                await_all(recv_sem, kept_back[t], kept.at[t, pl.ds(0, rows - 1)])
-                slope = lax.dot_general(
-                    residual.astype(BF16),
-                    kept[t].reshape(rows * KMAX, depth),
-                    NEAR,
-                    preferred_element_type=F32,
+                slope = jnp.dot(
+                    residual.astype(BF16), turned[t - 1], preferred_element_type=F32
                 ).astype(BF16)
                 for k in range(rows):
                     slope_send[t - 1, k] = slope[:, k * KMAX : (k + 1) * KMAX]
@@ -363,9 +362,12 @@
                 remote(mine, mine, peer, out, back).start()
             others = seen_all.at[t, pl.ds(0, high - 1)]
             lead_sent.append((out, lambda t=t: seen_all.at[t, pl.ds(0, high - 1)]))
+            if t < steps - 2:
+                await_all(recv_sem, kept_back[t + 1], kept.at[t + 1, pl.ds(0, rows - 1)])
+                turned[t] = kept[t + 1].reshape(rows * KMAX, depth).T
             await_all(recv_sem, back, others)
             residual = own_measured - jnp.sum(seen_all[t].astype(F32), axis=0)
-            energy.append(jnp.sum(residual * residual))
+            energy.append(jnp.sum(residual * residual, axis=0, keepdims=True))
 
         residual_all[y] = residual.astype(BF16)
         own = residual_all.at[y]
@@ -375,7 +377,7 @@
         lanes = iota((1, KMAX), 1)
         values = jnp.zeros((1, KMAX), F32)
         for t in range(steps):
-            values = jnp.where(lanes == t, energy[t], values)
+            values = jnp.where(lanes == t, jnp.sum(energy[t], axis=1, keepdims=True), values)
         energy_all[y] = values
         mine = energy_all.at[y]
         for peer in y_leads:
@@ -388,12 +390,12 @@
 
     z_out, x_out, near_z_out, near_x_out = (next(sending) for _ in range(4))
     near_back = [next(landing) for _ in range(chunks)]
-    rest_back = [next(landing) for _ in range(chunks)]
     first_by_x = list(range(along_x))
     across_first = list(range(along_x, chunks))
     order = []
     for n in range(max(len(first_by_x), len(across_first))):
-        order += first_by_x[n : n + 1] + across_first[n : n + 1]
+        pair = first_by_x[n : n + 1] + across_first[n : n + 1]
+        order += pair if n == 0 else pair[::-1]
 
     def send_dense(lhs, to_x, to_z, from_x, from_z, out_x, out_z, back):
         count = lhs.shape[0] // party
@@ -434,6 +436,23 @@
         residual_all[y], near_x, near_z, near_by_x, near_by_z, near_x_out, near_z_out, near_back
     )
 
+    pl.when(loop)(lambda: await_all(recv_sem, move_back, moved_recv.at[pl.ds(0, far - 1)]))
+    pl.when(no_loop)(lambda: await_all(recv_sem, move_back, moved_recv))
+    y_order = [y] + y_from
+    moved = split3(jnp.concatenate([moved_recv[yy] for yy in y_order], axis=0))
+    for c in order:
+        span = slice(c * chunk, (c + 1) * chunk)
+        carry_all[:, span] = add3(
+            jnp.dot(
+                moved,
+                one_hot(index_own[steps - 2], c * chunk, chunk).astype(BF16),
+                preferred_element_type=F32,
+            )
+        )
+        mask_all[:, span] = jnp.sum(
+            one_hot(index_own[steps - 1], c * chunk, chunk), axis=0, keepdims=True
+        )
+
     @pl.when(lead)
     def _():
         for n, yy in enumerate(y_from):
@@ -450,7 +469,7 @@
         rest_by_z,
         x_out,
         z_out,
-        rest_back,
+        near_back,
     )
 
     @pl.when(lead)
@@ -461,14 +480,15 @@
         lead_sent.append((total_out, lambda: energy_sum))
 
     rest = part * (far - 1)
+    both_x = kept_out.at[pl.ds(0, group), pl.ds(0, (pairs - 1) * chunk)]
+    both_z = kept_out.at[pl.ds(0, group), pl.ds(0, pairs * chunk // 2)]
     second = {}
     pair_out, line_out = next(sending), next(sending)
     for c in order:
         second[c] = next(landing)
         if c < along_x:
-            await_all(recv_sem, near_back[c], near_by_x.at[c])
+            await_all(recv_sem, near_back[c], both_x)
             near = near_x[c, x].astype(F32) + jnp.sum(near_by_x[c].astype(F32), axis=0)
-            await_all(recv_sem, rest_back[c], rest_by_x.at[c])
             total = rest_x[c, x].astype(F32) + jnp.sum(rest_by_x[c].astype(F32), axis=0)
             for k in range(2):
                 pair_send[c, k] = jnp.concatenate(
@@ -479,9 +499,8 @@
             ).start()
         else:
             n = c - along_x
-            await_all(recv_sem, near_back[c], near_by_z.at[n])
+            await_all(recv_sem, near_back[c], both_z)
             near = near_z[n, z].astype(F32) + near_by_z[n].astype(F32)
-            await_all(recv_sem, rest_back[c], rest_by_z.at[n])
             total = rest_z[n, z].astype(F32) + rest_by_z[n].astype(F32)
             for k in range(pairs):
                 line_send[n, k] = jnp.concatenate(
@@ -498,22 +517,17 @@
     sent.append((pair_out, pair_recv))
     sent.append((line_out, line_recv))
 
-    pl.when(follow)(lambda: await_all(recv_sem, total_back, energy_sum))
-    norm_all[i, :, width:] = energy_sum[...]
-    pl.when(loop)(lambda: await_all(recv_sem, move_back, moved_recv.at[pl.ds(0, far - 1)]))
-    pl.when(no_loop)(lambda: await_all(recv_sem, move_back, moved_recv))
-    y_order = [y] + y_from
-    moved = split3(jnp.concatenate([moved_recv[yy] for yy in y_order], axis=0))
-    for c in order:
+    norm_out, norm_back = [next(sending) for _ in range(2)], [next(landing) for _ in range(2)]
+    early = max(chunks - 2, 1) * chunk
+    spans = [pl.ds(0, early), pl.ds(early, width + KMAX - early)]
+
+    def share(n):
+        mine = norm_all.at[i, :, spans[n]]
+        for peer in row_peers:
+            remote(mine, mine, peer, norm_out[n], norm_back[n]).start()
+
+    for place, c in enumerate(order):
         span = slice(c * chunk, (c + 1) * chunk)
-        before = add3(
-            jnp.dot(
-                moved,
-                one_hot(index_own[steps - 2], c * chunk, chunk).astype(BF16),
-                preferred_element_type=F32,
-            )
-        )
-        mask = jnp.sum(one_hot(index_own[steps - 1], c * chunk, chunk), axis=0, keepdims=True)
         if c < along_x:
             await_all(recv_sem, second[c], pair_recv.at[c])
             gradient = pair_send[c, z].astype(F32) + pair_recv[c].astype(F32)
@@ -521,20 +535,28 @@
             n = c - along_x
             await_all(recv_sem, second[c], line_recv.at[n])
             gradient = line_send[n, x].astype(F32) + jnp.sum(line_recv[n].astype(F32), axis=0)
-        stepped = before + STEP_SIZE * gradient
-        settled = stepped * mask
+        stepped = carry_all[:, span] + STEP_SIZE * gradient
+        norm_all[i, :, place * chunk : (place + 1) * chunk] = jnp.sum(
+            stepped * stepped, axis=0, keepdims=True
+        )
+        if place == chunks - 1:
+            pl.when(follow)(lambda: await_all(recv_sem, total_back, energy_sum))
+            norm_all[i, :, width:] = energy_sum[...]
+            share(1)
+        elif (place + 1) * chunk == early:
+            share(0)
+        settled = stepped * mask_all[:, span]
         for n, yy in enumerate(y_order):
             kept_out[rows_of(0, yy), span] = settled[n * part : (n + 1) * part]
-        norm_all[i, :, span] = jnp.sum(stepped * stepped, axis=0, keepdims=True)
-
-    out, back = next(sending), next(landing)
-    mine = norm_all.at[i]
-    for peer in row_peers:
-        remote(mine, mine, peer, out, back).start()
-    others = norm_all.at[pl.ds(0, rows - 1)]
-    sent.append((out, others))
-    await_all(recv_sem, back, others)
-    sums_out[...] = jnp.sum(norm_all[...], axis=0)
+
+    for n in range(2):
+        others = norm_all.at[pl.ds(0, rows - 1), :, spans[n]]
+        sent.append((norm_out[n], others))
+        await_all(recv_sem, norm_back[n], others)
+    summed = jnp.sum(norm_all[...], axis=0)
+    for place, c in enumerate(order):
+        sums_out[:, c * chunk : (c + 1) * chunk] = summed[:, place * chunk : (place + 1) * chunk]
+    sums_out[:, width:] = summed[:, width:]
 
     pl.when(loop)(
         lambda: await_all(send_sem, first_out, first_send.at[pl.ds(0, far - 1)])
@@ -598,6 +620,7 @@
                 pltpu.VMEM((steps, KMAX, 1), jnp.int32),
                 pltpu.VMEM((turns, KMAX, 1), jnp.int32),
                 pltpu.VMEM((turns, rows, KMAX, depth), BF16),
+                pltpu.VMEM((turns - 1, depth, rows * KMAX), BF16),
                 pltpu.VMEM((far, party, KMAX), BF16),
                 pltpu.VMEM((rows, party, KMAX), BF16),
                 pltpu.VMEM((turns, rows, party, KMAX), BF16),
@@ -622,10 +645,12 @@
                 pltpu.VMEM((along_x, group, span), BF16),
                 pltpu.VMEM((along_z, pairs, group, span), BF16),
                 pltpu.VMEM((along_z, pairs - 1, group, span), BF16),
+                pltpu.VMEM((group, width), F32),
+                pltpu.VMEM((1, width), F32),
                 pltpu.VMEM((rows, 1, width + KMAX), F32),
                 pltpu.SemaphoreType.DMA((chunks + 2,)),
-                pltpu.SemaphoreType.DMA((24,)),
-                pltpu.SemaphoreType.DMA((21 + 3 * chunks,)),
+                pltpu.SemaphoreType.DMA((25,)),
+                pltpu.SemaphoreType.DMA((22 + 2 * chunks,)),
             ],
             compiler_params=pltpu.CompilerParams(
                 collective_id=0, has_side_effects=True, vmem_limit_bytes=40 * 2**20

time: 78.8 us -> 78.3 us (level)
  no operation moved by 1% of the time
where the time goes in v6:
time: 78.3 us; the launch traced here: 78.2 us
  Pallas kernels  77.6 us (99%)
    pallas_call x1, Pallas kernels, local(): pl.pallas_call(functools.partial(kernel, (rows, far, high, along_x)), out...  76.7 us

profile of v6, /device:TPU:32, one launch (start us, length us, event | category | flops | bytes accessed | tf_op | source)
XLA Modules:
  0.0 78.2 jit_solution(1669039484760455904)
XLA Ops:
  0.6 76.7 %shard_map.58 = (f32[32,4096]{1,0:T(8,128)S(1)}, f32[1,4224]{1,0:T(1,128)S(1)}) custom-call(s32[4,2048]{1,0:T(4,128)} %support_in.1, f32[256,512]{1,0:T(8,128)} %measured_in.1, bf16[512,4096]{1,0:T(8,128)(2,1)} %matrix.1), custom_call_target="tpu_custom_call" | custom-call | tf_op jit(solution)/shard_map/pallas_call | solution.py:608
  77.3 0.8 %shard_map.59 = (f32[32,4096]{1,0:T(8,128)}, f32[4096]{0:T(1024)}, f32[4]{0:T(128)}) custom-call(f32[32,4096]{1,0:T(8,128)S(1)} %get-tuple-element.5.kept, f32[1,4224]{1,0:T(1,128)S(1)} %get-tuple-element.6.sums), custom_call_target="tpu_custom_call" | custom-call | tf_op jit(solution)/shard_map/pallas_call | solution.py:659

commit v7 on v6

--- a/solution.py
+++ b/solution.py
@@ -259,7 +259,7 @@
 
     def spread(t):
         own = kept.at[t, q]
-        for peer in y_leads:
+        for peer in y_leads[::-1]:
             remote(own, own, peer, kept_out_sem[t], kept_back[t]).start()
         pl.when(follow)(lambda: remote(own, own, partner, kept_out_sem[t], kept_back[t]).start())
 

time: 78.3 us -> 77.7 us (level)
  no operation moved by 1% of the time
where the time goes in v7:
time: 77.7 us; the launch traced here: 77.6 us
  Pallas kernels  76.9 us (99%)
    pallas_call x1, Pallas kernels, local(): pl.pallas_call(functools.partial(kernel, (rows, far, high, along_x)), out...  76.1 us

profile of v7, /device:TPU:32, one launch (start us, length us, event | category | flops | bytes accessed | tf_op | source)
XLA Modules:
  0.0 77.6 jit_solution(7079048031911207354)
XLA Ops:
  0.6 76.1 %shard_map.58 = (f32[32,4096]{1,0:T(8,128)S(1)}, f32[1,4224]{1,0:T(1,128)S(1)}) custom-call(s32[4,2048]{1,0:T(4,128)} %support_in.1, f32[256,512]{1,0:T(8,128)} %measured_in.1, bf16[512,4096]{1,0:T(8,128)(2,1)} %matrix.1), custom_call_target="tpu_custom_call" | custom-call | tf_op jit(solution)/shard_map/pallas_call | solution.py:608
  76.7 0.8 %shard_map.59 = (f32[32,4096]{1,0:T(8,128)}, f32[4096]{0:T(1024)}, f32[4]{0:T(128)}) custom-call(f32[32,4096]{1,0:T(8,128)S(1)} %get-tuple-element.5.kept, f32[1,4224]{1,0:T(1,128)S(1)} %get-tuple-element.6.sums), custom_call_target="tpu_custom_call" | custom-call | tf_op jit(solution)/shard_map/pallas_call | solution.py:659
